TPU v7x, 32 devices: a whole 2x2x4 slice. The times are simulated.
32 devices in a mesh: rep: 2 (over x), dp: 16 (over y, z, core).
Axes of the slice: x: 2, y: 2, z: 4, core: 2. Of those that a mesh axis runs over, the one named last changes fastest.
Arguments:
- x: bfloat16 [32, 2048, 1024], P(('rep', 'dp')), parts along dimension 0
- dy: bfloat16 [32, 2048, 1024], P(('rep', 'dp')), parts along dimension 0
- w_gate: bfloat16 [2, 1024, 3328], P(None, 'dp')
- w_up: bfloat16 [2, 1024, 3328], P(None, 'dp')
- w_down: bfloat16 [2, 3328, 1024], P(None, 'dp')
- m_w_gate: float32 [2, 1024, 3328], P(None, 'dp')
- m_w_up: float32 [2, 1024, 3328], P(None, 'dp')
- m_w_down: float32 [2, 3328, 1024], P(None, 'dp')
- v_w_gate: float32 [2, 1024, 3328], P(None, 'dp')
- v_w_up: float32 [2, 1024, 3328], P(None, 'dp')
- v_w_down: float32 [2, 3328, 1024], P(None, 'dp')
Outputs:
- output 1: bfloat16 [4, 1024, 3328], P('rep', 'dp'), parts along dimension 0
- output 2: bfloat16 [4, 1024, 3328], P('rep', 'dp'), parts along dimension 0
- output 3: bfloat16 [4, 3328, 1024], P('rep', 'dp'), parts along dimension 0
- output 4: float32 [4, 1024, 3328], P('rep', 'dp'), parts along dimension 0
- output 5: float32 [4, 1024, 3328], P('rep', 'dp'), parts along dimension 0
- output 6: float32 [4, 3328, 1024], P('rep', 'dp'), parts along dimension 0
- output 7: float32 [4, 1024, 3328], P('rep', 'dp'), parts along dimension 0
- output 8: float32 [4, 1024, 3328], P('rep', 'dp'), parts along dimension 0
- output 9: float32 [4, 3328, 1024], P('rep', 'dp'), parts along dimension 0
There are 2 independent parts. A program takes and returns all parts, laid end to end along the dimension named above; an argument that names none is the same for every part.
All inputs are finite; a program needn't handle non-finite values.
Results may differ from a plain program's by a relative error of at most 0.022.
Values are sent between devices in bfloat16 or wider.
A program may use at most 2 GiB of HBM per device.

v0:
```python
import jax
import jax.numpy as jnp
from jax import lax
from jax.sharding import PartitionSpec as P

NAMES = ("w_gate", "w_up", "w_down")


def matmul(a, w):
    return jnp.dot(a, w, preferred_element_type=jnp.float32).astype(jnp.bfloat16)


def normed(h):
    wide = h.astype(jnp.float32)
    scale = lax.rsqrt(jnp.mean(wide**2, -1, keepdims=True) + 1e-6)
    return (wide * scale).astype(jnp.bfloat16)


def layer(h, w):
    a = normed(h)
    gate = jnp.dot(a, w["w_gate"], preferred_element_type=jnp.float32)
    up = jnp.dot(a, w["w_up"], preferred_element_type=jnp.float32)
    return h + matmul((jax.nn.silu(gate) * up).astype(jnp.bfloat16), w["w_down"])


def adamw(w, m, v, g):
    m = 0.9 * m + 0.1 * g
    v = 0.95 * v + 0.05 * g * g
    step = m * lax.rsqrt(v + 1e-8) + 0.1 * w
    return (w - 0.02 * step).astype(jnp.bfloat16), m, v


def clipped(gradients, sum_of_squares, count):
    factor = jnp.minimum(1.0, 0.5 * lax.rsqrt(sum_of_squares / count + 1e-30))
    return [g * factor for g in gradients]


def solution(mesh):
    def fetched(weights, number):
        return {name: lax.all_gather(w[number], "dp", axis=0, tiled=True) for name, w in zip(NAMES, weights, strict=True)}

    def step(x, dy, *arrays):
        weights, m, v = (arrays[i : i + 3] for i in (0, 3, 6))
        layers = weights[0].shape[0]
        h, kept = x[0], []
        for number in range(layers):
            kept.append(h)
            h = layer(h, fetched(weights, number))
        by_h, mine = dy[0], [None] * layers
        for number in reversed(range(layers)):
            _, back = jax.vjp(lambda w, h: layer(h, w), fetched(weights, number), kept[number])
            by_w, by_h = back(by_h)
            mine[number] = [lax.psum_scatter(by_w[name], "dp", scatter_dimension=0, tiled=True) for name in NAMES]
        gradients = [jnp.stack([mine[number][i] for number in range(layers)]).astype(jnp.float32) for i in range(3)]
        squares = lax.psum(sum(jnp.sum(g * g) for g in gradients), "dp")
        gradients = clipped(gradients, squares, lax.psum(1, "dp") * sum(g.size for g in gradients))
        new = [adamw(w.astype(jnp.float32), m, v, g) for w, m, v, g in zip(weights, m, v, gradients, strict=True)]
        return tuple(one[which] for which in range(3) for one in new)

    states, cut = P(("rep", "dp"), None, None), P(None, "dp", None)
    return jax.shard_map(
        step,
        mesh=mesh,
        in_specs=(states, states) + (cut,) * 9,
        out_specs=(P("rep", "dp", None),) * 9,
        check_vma=False,
    )
```

profile of v0, /device:TPU:0, one launch (start us, length us, event | category | flops | bytes accessed | tf_op | source)
XLA Modules:
  0.0 1120.5 jit_solution(1660301196352092733)
XLA Ops:
  15.5 6.5 copy.20
  25.1 6.5 copy.21
  31.6 46.2 %all-gather.13.cloned.1.call-done = bf16[1,1024,3328]{2,1,0:T(8,128)(2,1)} async-done(((bf16[1,64,3328]{2,1,0:T(8,128)(2,1)}), bf16[1,1024,3328]{2,1,0:T(8,128)(2,1)}) %all-gather.13.cloned.1.call-update) | async-done | bytes 6815760 | tf_op jit(solution)/shard_map/all_gather | solution.py:40
  77.8 23.2 %fusion.41 = f32[2048,3328]{1,0:T(8,128)} fusion(bf16[1,1024,3328]{2,1,0:T(8,128)(2,1)} %all-gather.13.cloned.1.call-done, bf16[1,2048,1024]{1,2,0:T(8,128)(2,1)} %copy.20, f32[2048]{0:T(1024)S(1)} %add_rsqrt_fusion), kind=kOutput, calls=%fused_computation.59 | convolution fusion | flops 13964935168 | bytes 38281216 | tf_op jit(solution)/shard_map/dot_general | solution.py:21
  101.0 43.1 %all-gather.15.cloned.1.call-done = bf16[1,1024,3328]{2,1,0:T(8,128)(2,1)} async-done(((bf16[1,64,3328]{2,1,0:T(8,128)(2,1)}), bf16[1,1024,3328]{2,1,0:T(8,128)(2,1)}) %all-gather.15.cloned.1.call-update) | async-done | bytes 6815760 | tf_op jit(solution)/shard_map/all_gather | solution.py:40
  144.2 32.1 %multiply_convert_fusion.1 = (bf16[2048,3328]{1,0:T(8,128)(2,1)}, f32[2048,3328]{1,0:T(8,128)}) fusion(f32[2048,3328]{1,0:T(8,128)} %fusion.41, bf16[1,1024,3328]{2,1,0:T(8,128)(2,1)} %all-gather.15.cloned.1.call-done, bf16[1,2048,1024]{1,2,0:T(8,128)(2,1)} %copy.20, f32[2048]{0:T(1024)S(1)} %add_rsqrt_fusion), kind=kOutput, calls=%fused_computation.17 | convolution fusion | flops 14005829632 | bytes 79175680 | tf_op jit(solution)/shard_map/dot_general | solution.py:22
  176.3 34.2 %all-gather.17.cloned.1.call-done = bf16[1,3328,1024]{2,1,0:T(8,128)(2,1)} async-done(((bf16[1,208,1024]{2,1,0:T(8,128)(2,1)}), bf16[1,3328,1024]{2,1,0:T(8,128)(2,1)}) %all-gather.17.cloned.1.call-update) | async-done | bytes 6815760 | tf_op jit(solution)/shard_map/all_gather | solution.py:40
  210.5 22.1 %fusion.19 = (f32[2048]{0:T(1024)S(1)}, bf16[2048,1024]{0,1:T(8,128)(2,1)}) fusion(bf16[2048,3328]{1,0:T(8,128)(2,1)} %get-tuple-element.24, bf16[1,3328,1024]{2,1,0:T(8,128)(2,1)} %all-gather.17.cloned.1.call-done, bf16[1,2048,1024]{1,2,0:T(8,128)(2,1)} %copy.20), kind=kOutput, calls=%fused_computation.37 | convolution fusion | flops 13969127424 | bytes 28844032 | tf_op jit(solution)/shard_map/dot_general | solution.py:10
  232.6 44.0 %all-gather.23.cloned.1.call-done = bf16[1,1024,3328]{2,1,0:T(8,128)(2,1)} async-done(((bf16[1,64,3328]{2,1,0:T(8,128)(2,1)}), bf16[1,1024,3328]{2,1,0:T(8,128)(2,1)}) %all-gather.23.cloned.1.call-update) | async-done | bytes 6815760 | tf_op jit(solution)/shard_map/all_gather | solution.py:40
  276.7 23.5 %fusion.28 = f32[2048,3328]{1,0:T(8,128)} fusion(bf16[1,1024,3328]{2,1,0:T(8,128)(2,1)} %all-gather.23.cloned.1.call-done, bf16[2048,1024]{0,1:T(8,128)(2,1)} %get-tuple-element.27, f32[2048]{0:T(1024)S(1)} %fusion.80), kind=kOutput, calls=%fused_computation.46 | convolution fusion | flops 13964935168 | bytes 38281216 | tf_op jit(solution)/shard_map/jvp()/dot_general | solution.py:22
  300.2 42.7 %all-gather.21.cloned.1.call-done = bf16[1,3328,1024]{2,1,0:T(8,128)(2,1)} async-done(((bf16[1,208,1024]{2,1,0:T(8,128)(2,1)}), bf16[1,3328,1024]{2,1,0:T(8,128)(2,1)}) %all-gather.21.cloned.1.call-update) | async-done | bytes 6815760 | tf_op jit(solution)/shard_map/all_gather | solution.py:40
  342.8 21.0 %convolution_convert_fusion.1 = bf16[2048,3328]{1,0:T(8,128)(2,1)} fusion(bf16[1,3328,1024]{2,1,0:T(8,128)(2,1)} %all-gather.21.cloned.1.call-done, bf16[1,2048,1024]{2,1,0:T(8,128)(2,1)} %param.12), kind=kOutput, calls=%fused_computation.23 | convolution fusion | flops 13965459456 | bytes 24641536 | tf_op jit(solution)/shard_map/transpose(jvp())/dot_general | solution.py:10
  363.8 45.2 %all-gather.19.cloned.1.call-done = bf16[1,1024,3328]{2,1,0:T(8,128)(2,1)} async-done(((bf16[1,64,3328]{2,1,0:T(8,128)(2,1)}), bf16[1,1024,3328]{2,1,0:T(8,128)(2,1)}) %all-gather.19.cloned.1.call-update) | async-done | bytes 6815760 | tf_op jit(solution)/shard_map/all_gather | solution.py:40
  409.0 39.6 %fusion.2 = (bf16[2048,3328]{1,0:T(8,128)(2,1)}, f32[2048,3328]{1,0:T(8,128)}) fusion(f32[2048,3328]{1,0:T(8,128)} %fusion.28, bf16[2048,3328]{1,0:T(8,128)(2,1)} %convolution_convert_fusion.1, bf16[1,1024,3328]{2,1,0:T(8,128)(2,1)} %all-gather.19.cloned.1.call-done, bf16[2048,1024]{0,1:T(8,128)(2,1)} %get-tuple-element.27, f32[2048]{0:T(1024)S(1)} %fusion.80), kind=kOutput, calls=%fused_computation.8 | convolution fusion | flops 14046724096 | bytes 92807168 | tf_op jit(solution)/shard_map/jvp()/dot_general | solution.py:21
  448.6 23.1 %fusion.12 = bf16[2048,1024]{0,1:T(8,128)(2,1)} fusion(bf16[2048,3328]{1,0:T(8,128)(2,1)} %convolution_convert_fusion.1, bf16[1,1024,3328]{2,1,0:T(8,128)(2,1)} %all-gather.23.cloned.1.call-done, f32[2048,3328]{1,0:T(8,128)} %get-tuple-element.29), kind=kOutput, calls=%fused_computation.21 | convolution fusion | flops 13999538176 | bytes 51904512 | tf_op jit(solution)/shard_map/transpose(jvp())/dot_general | solution.py:22
  471.8 21.7 %fusion.21 = (f32[2048]{0:T(1024)S(1)}, bf16[2048,1024]{0,1:T(8,128)(2,1)}) fusion(bf16[2048,1024]{0,1:T(8,128)(2,1)S(1)} %copy-done.1, bf16[2048,1024]{0,1:T(8,128)(2,1)} %fusion.12, bf16[2048,3328]{1,0:T(8,128)(2,1)} %get-tuple-element.28, bf16[1,1024,3328]{2,1,0:T(8,128)(2,1)} %all-gather.19.cloned.1.call-done), kind=kOutput, calls=%fused_computation.39 | convolution fusion | flops 13969127424 | bytes 33038336 | tf_op jit(solution)/shard_map/transpose(jvp())/dot_general | solution.py:21
  493.5 4.9 fusion.44
  500.4 19.6 %convolution_convert_fusion.2 = bf16[3328,1024]{1,0:T(8,128)(2,1)} fusion(bf16[2048,3328]{1,0:T(8,128)(2,1)} %get-tuple-element.24, bf16[2048,1024]{0,1:T(8,128)(2,1)S(1)} %fusion.44), kind=kOutput, calls=%fused_computation.44 | convolution fusion | flops 13962051584 | bytes 24641536 | tf_op jit(solution)/shard_map/transpose(jvp())/dot_general | solution.py:10
  520.0 27.4 %fusion.25 = bf16[3328,1024]{1,0:T(8,128)(2,1)} fusion(f32[2048,3328]{1,0:T(8,128)} %fusion.28, bf16[1,2048,1024]{2,1,0:T(8,128)(2,1)} %param.12, f32[2048,3328]{1,0:T(8,128)} %get-tuple-element.29), kind=kOutput, calls=%fused_computation.41 | convolution fusion | flops 14002946048 | bytes 65536000 | tf_op jit(solution)/shard_map/transpose(jvp())/dot_general | solution.py:10
  547.5 21.1 %convolution_convert_fusion = bf16[2048,3328]{1,0:T(8,128)(2,1)} fusion(bf16[2048,1024]{0,1:T(8,128)(2,1)} %copy-done.2, bf16[1,3328,1024]{2,1,0:T(8,128)(2,1)} %all-gather.17.cloned.1.call-done), kind=kOutput, calls=%fused_computation.22 | convolution fusion | flops 13965459456 | bytes 24641536 | tf_op jit(solution)/shard_map/transpose(jvp())/dot_general | solution.py:10
  568.6 25.6 %fusion.27 = bf16[1024,3328]{1,0:T(8,128)(2,1)} fusion(bf16[2048,3328]{1,0:T(8,128)(2,1)} %convolution_convert_fusion, f32[2048,3328]{1,0:T(8,128)} %fusion.41, bf16[1,2048,1024]{1,2,0:T(8,128)(2,1)} %copy.20, f32[2048]{0:T(1024)S(1)} %copy-done.19), kind=kOutput, calls=%fused_computation.43 | convolution fusion | flops 14009237504 | bytes 51912704 | tf_op jit(solution)/shard_map/transpose(jvp())/dot_general | solution.py:22
  594.9 25.3 %fusion.26 = bf16[1024,3328]{1,0:T(8,128)(2,1)} fusion(bf16[2048,3328]{1,0:T(8,128)(2,1)} %convolution_convert_fusion.1, bf16[2048,1024]{0,1:T(8,128)(2,1)} %get-tuple-element.27, f32[2048]{0:T(1024)S(1)} %copy-done.15, f32[2048,3328]{1,0:T(8,128)} %get-tuple-element.29), kind=kOutput, calls=%fused_computation.42 | convolution fusion | flops 14009237504 | bytes 51912704 | tf_op jit(solution)/shard_map/transpose(jvp())/dot_general | solution.py:22
  620.3 31.2 %fusion.22 = bf16[1024,3328]{1,0:T(8,128)(2,1)} fusion(f32[2048,3328]{1,0:T(8,128)} %fusion.41, f32[2048,3328]{1,0:T(8,128)} %get-tuple-element.25, bf16[2048,3328]{1,0:T(8,128)(2,1)} %convolution_convert_fusion, bf16[1,2048,1024]{1,2,0:T(8,128)(2,1)} %copy.20, f32[2048]{0:T(1024)S(1)} %copy-done.19), kind=kOutput, calls=%fused_computation.40 | convolution fusion | flops 14043316224 | bytes 79175680 | tf_op jit(solution)/shard_map/transpose(jvp())/dot_general | solution.py:21
  651.6 21.3 %convolution_convert_fusion.3 = bf16[1024,3328]{1,0:T(8,128)(2,1)} fusion(bf16[2048,3328]{1,0:T(8,128)(2,1)} %get-tuple-element.28, bf16[2048,1024]{0,1:T(8,128)(2,1)} %get-tuple-element.27, f32[2048]{0:T(1024)S(1)} %copy-done.15), kind=kOutput, calls=%fused_computation.45 | convolution fusion | flops 13964935168 | bytes 24649728 | tf_op jit(solution)/shard_map/transpose(jvp())/dot_general | solution.py:21
  672.9 26.9 %reduce-scatter.17.cloned.1.call-done = bf16[208,1024]{1,0:T(8,128)(2,1)} async-done(((bf16[3328,1024]{1,0:T(8,128)(2,1)}), bf16[208,1024]{1,0:T(8,128)(2,1)}) %reduce-scatter.17.cloned.1.call-update) | async-done | bytes 426000 | tf_op jit(solution)/shard_map/reduce_scatter | solution.py:53
  702.0 89.6 %reduce-scatter.11.cloned.1.call-done = bf16[64,3328]{1,0:T(8,128)(2,1)} async-done(((bf16[1024,3328]{1,0:T(8,128)(2,1)}), bf16[64,3328]{1,0:T(8,128)(2,1)}) %reduce-scatter.11.cloned.1.call-update) | async-done | bytes 426000 | tf_op jit(solution)/shard_map/reduce_scatter | solution.py:53
  791.6 91.6 %reduce-scatter.13.cloned.1.call-done = bf16[64,3328]{1,0:T(8,128)(2,1)} async-done(((bf16[1024,3328]{1,0:T(8,128)(2,1)}), bf16[64,3328]{1,0:T(8,128)(2,1)}) %reduce-scatter.13.cloned.1.call-update) | async-done | bytes 426000 | tf_op jit(solution)/shard_map/reduce_scatter | solution.py:53
  885.5 89.5 %reduce-scatter.7.cloned.1.call-done = bf16[64,3328]{1,0:T(8,128)(2,1)} async-done(((bf16[1024,3328]{1,0:T(8,128)(2,1)}), bf16[64,3328]{1,0:T(8,128)(2,1)}) %reduce-scatter.7.cloned.1.call-update) | async-done | bytes 426000 | tf_op jit(solution)/shard_map/reduce_scatter | solution.py:53
  975.0 91.6 %reduce-scatter.9.cloned.1.call-done = bf16[64,3328]{1,0:T(8,128)(2,1)} async-done(((bf16[1024,3328]{1,0:T(8,128)(2,1)}), bf16[64,3328]{1,0:T(8,128)(2,1)}) %reduce-scatter.9.cloned.1.call-update) | async-done | bytes 426000 | tf_op jit(solution)/shard_map/reduce_scatter | solution.py:53
  1070.7 31.5 %psum.7 = f32[]{:T(128)} all-reduce(f32[]{:T(128)S(6)} %add.99), channel_id=1, replica_groups=mesh['rep'=2,'dp'=16] {'dp'}, use_global_device_ids=true, to_apply=%region_12.13 | all-reduce | flops 1 | bytes 8 | tf_op jit(solution)/shard_map/psum | solution.py:55
  1103.0 5.0 fusion.76
  1108.9 4.3 fusion.67
  (75 shorter events, 21.7 us)
Async XLA Ops:
  7.2 70.7 %all-gather.13.cloned.1.call-start = ((), (), s32[]{:S(2)}) async-start(), calls=%async_computation.12 | async-start | bytes 7241728 | tf_op jit(solution)/shard_map/all_gather | solution.py:40
  9.3 134.8 %all-gather.15.cloned.1.call-start = ((), (), s32[]{:S(2)}) async-start(), calls=%async_computation.13 | async-start | bytes 7241728 | tf_op jit(solution)/shard_map/all_gather | solution.py:40
  11.5 199.0 %all-gather.17.cloned.1.call-start = ((), (), s32[]{:S(2)}) async-start(), calls=%async_computation.14 | async-start | bytes 7241728 | tf_op jit(solution)/shard_map/all_gather | solution.py:40
  13.7 263.0 %all-gather.23.cloned.1.call-start = ((), (), s32[]{:S(2)}) async-start(), calls=%async_computation.17 | async-start | bytes 7241728 | tf_op jit(solution)/shard_map/all_gather | solution.py:40
  14.2 328.6 %all-gather.21.cloned.1.call-start = ((), (), s32[]{:S(2)}) async-start(), calls=%async_computation.16 | async-start | bytes 7241728 | tf_op jit(solution)/shard_map/all_gather | solution.py:40
  14.8 394.2 %all-gather.19.cloned.1.call-start = ((), (), s32[]{:S(2)}) async-start(), calls=%async_computation.15 | async-start | bytes 7241728 | tf_op jit(solution)/shard_map/all_gather | solution.py:40
  15.4 657.5 %reduce-scatter.15.cloned.1.call-start = ((), (), s32[]{:S(2)}) async-start(), calls=%async_computation.10 | async-start | bytes 7241728 | tf_op jit(solution)/shard_map/reduce_scatter | solution.py:53
  25.1 119.1 %copy-start.18 = (f32[2048]{0:T(1024)}, f32[2048]{0:T(1024)S(1)}, u32[]{:S(2)}) copy-start(f32[2048]{0:T(1024)S(1)} %add_rsqrt_fusion) | copy-start | bytes 24580
  232.6 67.5 %copy-start.16 = (f32[2048]{0:T(1024)}, f32[2048]{0:T(1024)S(1)}, u32[]{:S(2)}) copy-start(f32[2048]{0:T(1024)S(1)} %get-tuple-element.26) | copy-start | bytes 24580
  232.6 260.9 %copy-start.14 = (f32[2048]{0:T(1024)}, f32[2048]{0:T(1024)S(1)}, u32[]{:S(2)}) copy-start(f32[2048]{0:T(1024)S(1)} %fusion.80) | copy-start | bytes 24580
  448.6 23.1 %copy-start.1 = (bf16[2048,1024]{0,1:T(8,128)(2,1)S(1)}, bf16[2048,1024]{0,1:T(8,128)(2,1)}, u32[]{:S(2)}) copy-start(bf16[2048,1024]{0,1:T(8,128)(2,1)} %get-tuple-element.27) | copy-start | bytes 12582916
  471.8 21.7 %copy-start.17 = (f32[2048]{0:T(1024)S(1)}, f32[2048]{0:T(1024)}, u32[]{:S(2)}) copy-start(f32[2048]{0:T(1024)} %copy-done.16) | copy-start | bytes 24580
  471.8 21.8 %copy-start = (bf16[1,2048,1024]{1,2,0:T(8,128)(2,1)S(1)}, bf16[1,2048,1024]{1,2,0:T(8,128)(2,1)}, u32[]{:S(2)}) copy-start(bf16[1,2048,1024]{1,2,0:T(8,128)(2,1)} %copy.21) | copy-start | bytes 12582916
  498.4 1.9 copy-start.2
  520.0 179.8 %reduce-scatter.17.cloned.1.call-start = ((), (), s32[]{:S(2)}) async-start(), calls=%async_computation.11 | async-start | bytes 7241728 | tf_op jit(solution)/shard_map/reduce_scatter | solution.py:53
  547.4 21.1 %copy-start.19 = (f32[2048]{0:T(1024)S(1)}, f32[2048]{0:T(1024)}, u32[]{:S(2)}) copy-start(f32[2048]{0:T(1024)} %copy-done.18) | copy-start | bytes 24580
  547.5 244.1 %reduce-scatter.11.cloned.1.call-start = ((), (), s32[]{:S(2)}) async-start(), calls=%async_computation.8 | async-start | bytes 7241728 | tf_op jit(solution)/shard_map/reduce_scatter | solution.py:53
  594.2 0.7 copy-start.15
  594.3 289.0 %reduce-scatter.13.cloned.1.call-start = ((), (), s32[]{:S(2)}) async-start(), calls=%async_computation.9 | async-start | bytes 7241728 | tf_op jit(solution)/shard_map/reduce_scatter | solution.py:53
  620.3 354.8 %reduce-scatter.7.cloned.1.call-start = ((), (), s32[]{:S(2)}) async-start(), calls=%async_computation.6 | async-start | bytes 7241728 | tf_op jit(solution)/shard_map/reduce_scatter | solution.py:53
  651.6 415.1 %reduce-scatter.9.cloned.1.call-start = ((), (), s32[]{:S(2)}) async-start(), calls=%async_computation.7 | async-start | bytes 7241728 | tf_op jit(solution)/shard_map/reduce_scatter | solution.py:53
  672.9 430.0 %copy-start.3 = (bf16[2,208,1024]{2,1,0:T(8,128)(2,1)S(1)}, bf16[2,208,1024]{2,1,0:T(8,128)(2,1)}, u32[]{:S(2)}) copy-start(bf16[2,208,1024]{2,1,0:T(8,128)(2,1)} %param.15) | copy-start | bytes 2555908
  672.9 435.1 %copy-start.4 = (bf16[2,64,3328]{2,1,0:T(8,128)(2,1)S(1)}, bf16[2,64,3328]{2,1,0:T(8,128)(2,1)}, u32[]{:S(2)}) copy-start(bf16[2,64,3328]{2,1,0:T(8,128)(2,1)} %param.13) | copy-start | bytes 2555908
  672.9 435.1 %copy-start.5 = (bf16[2,64,3328]{2,1,0:T(8,128)(2,1)S(1)}, bf16[2,64,3328]{2,1,0:T(8,128)(2,1)}, u32[]{:S(2)}) copy-start(bf16[2,64,3328]{2,1,0:T(8,128)(2,1)} %param.14) | copy-start | bytes 2555908
  791.6 316.4 %copy-start.6 = (bf16[64,3328]{1,0:T(8,128)(2,1)S(1)}, bf16[64,3328]{1,0:T(8,128)(2,1)}, u32[]{:S(2)}) copy-start(bf16[64,3328]{1,0:T(8,128)(2,1)} %reduce-scatter.11.cloned.1.call-done) | copy-start | bytes 1277956
  883.2 224.8 %copy-start.7 = (bf16[64,3328]{1,0:T(8,128)(2,1)S(1)}, bf16[64,3328]{1,0:T(8,128)(2,1)}, u32[]{:S(2)}) copy-start(bf16[64,3328]{1,0:T(8,128)(2,1)} %reduce-scatter.13.cloned.1.call-done) | copy-start | bytes 1277956
  1102.9 5.1 copy-start.8
  1102.9 5.1 copy-start.9
  1102.9 5.1 copy-start.10
  1102.9 5.1 copy-start.11
  1102.9 5.1 copy-start.12
  1103.0 6.0 copy-start.13
Sparse Core Ops, SparseCore 0:
  10.9 66.9 all-gather.12
  80.7 63.3 all-gather.14
  147.1 63.3 all-gather.16
  213.2 63.3 all-gather.22
  279.4 63.3 all-gather.20
  345.6 63.3 all-gather.18
  520.1 87.8 reduce-scatter.14
  612.0 87.7 reduce-scatter.16
  703.8 87.7 reduce-scatter.10
  795.4 87.7 reduce-scatter.12
  887.2 87.7 reduce-scatter.6
  978.8 87.7 reduce-scatter.8
where the time goes:
time: 1130 us; the launch traced here: 1120 us
  waiting for transfers between devices  646 us (57%)
  matrix products  378 us (33%)
  blocking collectives  31.5 us (3%)
  other arithmetic  23.9 us (2%)
  local copies, waits for them, and re-layouts  22.8 us (2%)
  between operations  17.5 us (2%)
    reduce_scatter x6, waiting for transfers between devices, step(): lax.psum_scatter(by_w[name], 'dp', scatter_dimension=0, tiled=True)  389 us
    all_gather x6, waiting for transfers between devices, fetched(): lax.all_gather(w[number], 'dp', axis=0, tiled=True)  255 us
    dot_general x5, matrix products, layer(): gate = jnp.dot(a, w['w_gate'], preferred_element_type=jnp.float32)  137 us
    dot_general x5, matrix products, layer(): up = jnp.dot(a, w['w_up'], preferred_element_type=jnp.float32)  130 us
    dot_general x5, matrix products, matmul(): jnp.dot(a, w, preferred_element_type=jnp.float32).astype(jnp.bfloat16)  111 us
    psum x1, blocking collectives, step(): squares = lax.psum(sum((jnp.sum(g * g) for g in gradients)), 'dp')  31.5 us
  transfers between devices with their start and end apart: 12, of which 11 were waited for; matrix products, arithmetic and copies ran while one was open for 27% of the time, Pallas kernels for 0%

commit v1 on v0

v1 whole, which is shorter than its diff:
```python
import functools

import jax
import jax.numpy as jnp
from jax import lax
from jax.experimental import pallas as pl
from jax.experimental.pallas import tpu as pltpu
from jax.sharding import PartitionSpec as P

BF16, F32 = jnp.bfloat16, jnp.float32
MIB = 1 << 20
CHIPS = 8
ANY = pl.BlockSpec(memory_space=pl.ANY)


def order(q):
    return q + lax.div(q, 4) * (11 - 2 * q)


class Here:
    def __init__(self):
        me = lax.axis_index("dp")
        self.me, self.c = me, lax.rem(me, 2)
        self.p = order(lax.div(me, 2))
        self.sibling = {"dp": 2 * lax.div(me, 2) + 1 - self.c}
        self.hops = (4 - self.c, 3 + self.c)
        self.next = tuple({"dp": 2 * self.chip(o) + self.c} for o in (1, CHIPS - 1))

    def chip(self, offset):
        return order(lax.rem(self.p + offset, CHIPS))


def remote(src, dst, send, recv, to):
    return pltpu.make_async_remote_copy(src, dst, send, recv, device_id=to, device_id_type=pl.DeviceIdType.MESH)


def greet(here):
    barrier = pltpu.get_barrier_semaphore()
    for to in (here.sibling, *here.next):
        pl.semaphore_signal(barrier, inc=1, device_id=to, device_id_type=pl.DeviceIdType.MESH)
    pl.semaphore_wait(barrier, 3)


class Gather:
    def __init__(self, shapes, cuts):
        self.shapes, self.cuts = shapes, cuts
        self.units = [(m, i, shape[0], shape[1] // cuts) for m, shape in enumerate(shapes) for i in range(cuts)]
        n = len(self.units)
        self.rounds = 5 * n
        dma = pltpu.SemaphoreType.DMA
        self.scratch = [dma((n, 2, 4)), dma((n, 2, 4)), dma((n, CHIPS)), dma((n, CHIPS)), dma((len(shapes),))]
        self.scratch += [pltpu.VMEM(shape, BF16) for shape in shapes]
        self.out_shapes = [jax.ShapeDtypeStruct((2 * CHIPS * r, c), BF16) for r, c in shapes]

    def bind(self, ins, outs, scratch):
        self.ins, self.outs = ins, outs
        self.send, self.recv, self.dsend, self.drecv, self.local = scratch[:5]
        self.held = scratch[5:]

    def block(self, here, u, offset, core):
        m, i, rows, cols = self.units[u]
        start = pl.multiple_of((2 * here.chip(offset) + core) * rows, 16)
        return self.outs[m].at[pl.ds(start, rows), pl.ds(i * cols, cols)]

    def own(self, u):
        m, i, rows, cols = self.units[u]
        return self.ins[m].at[:, pl.ds(i * cols, cols)]

    def start(self, here):
        greet(here)
        for m in range(len(self.shapes)):
            pltpu.make_async_copy(self.ins[m], self.held[m], self.local.at[m]).start()

    def unit(self, here, u, h):
        @pl.when(h == 0)
        def _():
            mine, dst = self.own(u), self.block(here, u, 0, here.c)
            for d in range(2):
                remote(mine, dst, self.send.at[u, d, 0], self.recv.at[u, d, 0], here.next[d]).start()
            remote(mine, dst, self.dsend.at[u, 0], self.drecv.at[u, 0], here.sibling).start()

        for d in range(2):
            offset = lax.rem(CHIPS - h, CHIPS) if d == 0 else h
            blk = self.block(here, u, offset, here.c)

            @pl.when((h >= 1) & (h <= here.hops[d]))
            def _():
                remote(blk, blk, self.send.at[u, d, h - 1], self.recv.at[u, d, h - 1], here.next[d]).wait_recv()

            @pl.when((h >= 1) & (h < here.hops[d]))
            def _():
                remote(blk, blk, self.send.at[u, d, h], self.recv.at[u, d, h], here.next[d]).start()

            @pl.when((h >= 1) & (h <= here.hops[d]))
            def _():
                remote(blk, blk, self.dsend.at[u, offset], self.drecv.at[u, offset], here.sibling).start()

    def round(self, here, r):
        n = len(self.units)
        for u in range(n):
            pl.when(lax.rem(r, n) == u)(functools.partial(self.unit, here, u, lax.div(r, n)))

    def finish(self, here):
        for m, (rows, cols) in enumerate(self.shapes):
            mine = self.outs[m].at[pl.ds(pl.multiple_of(here.me * rows, 16), rows), :]
            pltpu.make_async_copy(self.ins[m], self.held[m], self.local.at[m]).wait()
            pltpu.make_async_copy(self.held[m], mine, self.local.at[m]).start()
        for u in range(len(self.units)):

            @pl.loop(0, CHIPS)
            def _(o):
                blk = self.block(here, u, o, here.c)
                remote(blk, blk, self.dsend.at[u, o], self.drecv.at[u, o], here.sibling).wait()

            for d in range(2):

                @pl.loop(0, here.hops[d])
                def _(h):
                    blk = self.block(here, u, 0, here.c)
                    remote(blk, blk, self.send.at[u, d, h], self.recv.at[u, d, h], here.next[d]).wait_send()

        for m, (rows, cols) in enumerate(self.shapes):
            mine = self.outs[m].at[pl.ds(pl.multiple_of(here.me * rows, 16), rows), :]
            pltpu.make_async_copy(self.held[m], mine, self.local.at[m]).wait()


class Scatter:
    def __init__(self, shapes, cuts):
        self.shapes, self.cuts = shapes, cuts
        self.units = [(m, i, shape[0], shape[1] // cuts) for m, shape in enumerate(shapes) for i in range(cuts)]
        n = len(self.units)
        self.rounds = 5 * n
        dma = pltpu.SemaphoreType.DMA
        self.scratch = [dma((n, 2, 4)), dma((n, 2, 4)), dma((n, CHIPS)), dma((n, CHIPS)), dma((n, CHIPS))]
        for _, _, rows, cols in self.units:
            self.scratch += [pltpu.VMEM((CHIPS, rows, cols), BF16)] * 2 + [pltpu.VMEM((2, 4, rows, cols), BF16)]
        self.scratch += [pltpu.VMEM(shape, BF16) for shape in shapes] + [dma((len(shapes),))]
        self.out_shapes = [jax.ShapeDtypeStruct(shape, BF16) for shape in shapes]

    def bind(self, ins, outs, scratch):
        self.ins, self.outs = ins, outs
        self.send, self.recv, self.dsend, self.drecv, self.local = scratch[:5]
        n = len(self.units)
        self.mine, self.theirs, self.came = (scratch[5 + j : 5 + 3 * n : 3] for j in range(3))
        self.total = scratch[5 + 3 * n : -1]
        self.put = scratch[-1]

    def term(self, here, u, offset, core):
        m, i, rows, cols = self.units[u]
        start = pl.multiple_of((2 * here.chip(offset) + core) * rows, 16)
        return self.ins[m].at[pl.ds(start, rows), pl.ds(i * cols, cols)]

    def fetch(self, here, u, o):
        return pltpu.make_async_copy(self.term(here, u, o, here.c), self.mine[u].at[o], self.local.at[u, o])

    def give(self, here, u, o):
        term = self.term(here, u, o, 1 - here.c)
        return remote(term, self.theirs[u].at[o], self.dsend.at[u, o], self.drecv.at[u, o], here.sibling)

    def start(self, here):
        greet(here)

        @pl.loop(0, CHIPS)
        def _(j):
            odd, half = lax.rem(j, 2), lax.div(j, 2)
            o = lax.rem((1 - odd) * (4 - half) + odd * (5 + half), CHIPS)
            for u in range(len(self.units)):
                self.give(here, u, o).start()
                self.fetch(here, u, o).start()

    def unit(self, here, u, k):
        m, i, rows, cols = self.units[u]
        mine, theirs, came = self.mine[u], self.theirs[u], self.came[u]
        for d in range(2):
            far = here.hops[d] - k
            o = far if d == 0 else CHIPS - far

            @pl.when(k < here.hops[d])
            def _():
                self.fetch(here, u, o).wait()
                self.give(here, u, o).wait_recv()

            @pl.when((k < here.hops[d]) & (k == 0))
            def _():
                mine[o] = (mine[o].astype(F32) + theirs[o].astype(F32)).astype(BF16)

            @pl.when((k < here.hops[d]) & (k > 0))
            def _():
                remote(mine.at[o], came.at[d, k - 1], self.send.at[u, d, k - 1], self.recv.at[u, d, k - 1], here.next[d]).wait_recv()
                mine[o] = (mine[o].astype(F32) + theirs[o].astype(F32) + came[d, k - 1].astype(F32)).astype(BF16)

            @pl.when(k < here.hops[d])
            def _():
                remote(mine.at[o], came.at[d, k], self.send.at[u, d, k], self.recv.at[u, d, k], here.next[d]).start()

        @pl.when(k == 4)
        def _():
            self.fetch(here, u, 0).wait()
            self.give(here, u, 0).wait_recv()
            total = mine[0].astype(F32) + theirs[0].astype(F32)
            for d in range(2):
                last = here.hops[d] - 1
                remote(mine.at[0], came.at[d, last], self.send.at[u, d, last], self.recv.at[u, d, last], here.next[d]).wait_recv()
                total += came[d, last].astype(F32)
            self.total[m][:, pl.ds(i * cols, cols)] = total.astype(BF16)

    def round(self, here, r):
        n = len(self.units)
        for u in range(n):
            pl.when(lax.rem(r, n) == u)(functools.partial(self.unit, here, u, lax.div(r, n)))

    def finish(self, here):
        for m in range(len(self.shapes)):
            pltpu.make_async_copy(self.total[m], self.outs[m], self.put.at[m]).start()
        for u in range(len(self.units)):

            @pl.loop(0, CHIPS)
            def _(o):
                self.give(here, u, o).wait_send()

            for d in range(2):

                @pl.loop(0, here.hops[d])
                def _(k):
                    remote(
                        self.mine[u].at[0], self.came[u].at[d, k], self.send.at[u, d, k], self.recv.at[u, d, k], here.next[d]
                    ).wait_send()

        for m in range(len(self.shapes)):
            pltpu.make_async_copy(self.total[m], self.outs[m], self.put.at[m]).wait()


def hosted(name, body, steps, marks, in_specs, out_specs, out_shape, args, carried=None, carried_args=(), number=None, scratch=(), limit=60):
    n_in, n_out, n_scratch = len(in_specs), len(out_specs), len(scratch)
    n_cin = len(carried_args)
    c_out = carried.out_shapes if carried else []

    def kernel(*refs):
        ins, refs = refs[:n_in], refs[n_in:]
        cin, refs = refs[:n_cin], refs[n_cin:]
        outs, refs = refs[:n_out], refs[n_out:]
        couts, refs = refs[: len(c_out)], refs[len(c_out) :]
        own, refs = refs[:n_scratch], refs[n_scratch:]
        step = pl.program_id(0)
        if carried is None:
            body(ins, outs, own, lambda j: None)
            return
        here = Here()
        carried.bind(cin, couts, refs)
        pl.when(step == 0)(functools.partial(carried.start, here))
        total = steps * marks

        def mark(j):
            at = step * marks + j

            @pl.loop(lax.div(at * carried.rounds, total), lax.div((at + 1) * carried.rounds, total))
            def _(r):
                carried.round(here, r)

        if body is None:
            mark(0)
        else:
            body(ins, outs, own, mark)
        pl.when(step == steps - 1)(functools.partial(carried.finish, here))

    params = dict(vmem_limit_bytes=limit * MIB, dimension_semantics=("arbitrary",))
    if carried is not None:
        params |= dict(collective_id=number, has_side_effects=True)
    out = pl.pallas_call(
        kernel,
        grid=(steps,),
        in_specs=[*in_specs, *[ANY] * n_cin],
        out_specs=[*out_specs, *[ANY] * len(c_out)],
        out_shape=[*out_shape, *c_out],
        scratch_shapes=[*scratch, *(carried.scratch if carried else [])],
        compiler_params=pltpu.CompilerParams(**params),
        name=name,
    )(*args, *carried_args)
    return out[:n_out], out[n_out:]


def whole(shape):
    return pl.BlockSpec(shape, lambda i: (0, 0), pipeline_mode=pl.Buffered(1))


def dot(a, b, over):
    return lax.dot_general(a, b, ((over[:1], over[1:]), ((), ())), preferred_element_type=F32)


def scaled(h):
    wide = h.astype(F32)
    return (wide * lax.rsqrt(jnp.mean(wide * wide, -1, keepdims=True) + 1e-6)).astype(BF16)


def up_kernel(a, wg, wu, **carry):
    t, d = a.shape
    ff = wg.shape[1]
    n, part = 256, 512

    def body(ins, outs, own, mark):
        a, wg, wu = ins
        act, s, v = outs
        for j in range(t // part):
            rows = pl.ds(j * part, part)
            g = dot(a[rows, :], wg[...], (1, 0))
            u = dot(a[rows, :], wu[...], (1, 0))
            sig = jax.nn.sigmoid(g)
            sl = g * sig
            act[rows, :] = (sl * u).astype(BF16)
            s[rows, :] = sl
            v[rows, :] = u * (sig * (1.0 + g * (1.0 - sig)))
            mark(j)

    col = lambda rows: pl.BlockSpec((rows, n), lambda i: (0, i))
    return hosted(
        "up", body, ff // n, t // part, [whole((t, d)), col(d), col(d)], [col(t)] * 3,
        [jax.ShapeDtypeStruct((t, ff), x) for x in (BF16, F32, F32)], (a, wg, wu), **carry,
    )


def down_kernel(act, wd, h, **carry):
    t, ff = act.shape
    d = wd.shape[1]
    m, n = 512, 256

    def body(ins, outs, own, mark):
        act, wd, h = ins
        new, a = outs
        for j in range(d // n):
            cols = pl.ds(j * n, n)
            new[:, cols] = h[:, cols] + dot(act[...], wd[:, cols], (1, 0)).astype(BF16)
            mark(j)
        a[...] = scaled(new[...])

    row = lambda cols: pl.BlockSpec((m, cols), lambda i: (i, 0))
    return hosted(
        "down", body, t // m, d // n, [row(ff), whole((ff, d)), row(d)], [row(d)] * 2,
        [jax.ShapeDtypeStruct((t, d), BF16)] * 2, (act, wd, h), **carry,
    )


def back_kernel(at, dh, wd, act, s, v, keep, **carry):
    d, t = at.shape
    ff = act.shape[1]
    n, part = 256, 512

    def body(ins, outs, own, mark):
        at, dh, wd, act, s, v = ins
        by_g, by_u, by_wd, by_wg, by_wu = outs if keep else (*own, *outs)
        for j in range(t // part):
            rows = pl.ds(j * part, part)
            by_act = dot(dh[rows, :], wd[...], (1, 1)).astype(BF16).astype(F32)
            by_g[rows, :] = (by_act * v[rows, :]).astype(BF16)
            by_u[rows, :] = (by_act * s[rows, :]).astype(BF16)
        mark(0)
        by_wd[...] = dot(act[...], dh[...], (0, 0)).astype(BF16)
        mark(1)
        by_wg[...] = dot(at[...], by_g[...], (1, 0)).astype(BF16)
        mark(2)
        by_wu[...] = dot(at[...], by_u[...], (1, 0)).astype(BF16)
        mark(3)

    col = lambda rows: pl.BlockSpec((rows, n), lambda i: (0, i))
    row = pl.BlockSpec((n, d), lambda i: (i, 0))
    shape = lambda *s: jax.ShapeDtypeStruct(s, BF16)
    return hosted(
        "back", body, ff // n, 4, [whole((d, t)), whole((t, d)), row, col(t), col(t), col(t)],
        [col(t)] * (2 * keep) + [row, col(d), col(d)],
        [shape(t, ff)] * (2 * keep) + [shape(ff, d), shape(d, ff), shape(d, ff)],
        (at, dh, wd, act, s, v), scratch=() if keep else [pltpu.VMEM((t, n), BF16)] * 2, **carry,
    )


def through_kernel(by_g, by_u, wg, wu, h, dh, **carry):
    t, ff = by_g.shape
    d = wg.shape[0]
    m, n = 256, 256

    def body(ins, outs, own, mark):
        by_g, by_u, wg, wu, h, dh = ins
        (new,) = outs
        (by_a,) = own
        for j in range(d // n):
            cols = pl.ds(j * n, n)
            one = dot(by_g[...], wg[cols, :], (1, 1)).astype(BF16)
            two = dot(by_u[...], wu[cols, :], (1, 1)).astype(BF16)
            by_a[:, cols] = (one + two).astype(F32)
            mark(j)
        wide, by = h[...].astype(F32), by_a[...]
        scale = lax.rsqrt(jnp.mean(wide * wide, -1, keepdims=True) + 1e-6)
        inner = jnp.mean(wide * by, -1, keepdims=True)
        new[...] = dh[...] + (by * scale - wide * (scale * scale * scale * inner)).astype(BF16)

    row = lambda cols: pl.BlockSpec((m, cols), lambda i: (i, 0))
    return hosted(
        "through", body, t // m, d // n, [row(ff), row(ff), whole((d, ff)), whole((d, ff)), row(d), row(d)], [row(d)],
        [jax.ShapeDtypeStruct((t, d), BF16)], (by_g, by_u, wg, wu, h, dh), scratch=[pltpu.VMEM((m, d), F32)], **carry,
    )


def alone(name, **carry):
    return hosted(name, None, 1, 1, [], [], [], (), **carry)[1]


def adamw(w, m, v, g):
    m = 0.9 * m + 0.1 * g
    v = 0.95 * v + 0.05 * g * g
    step = m * lax.rsqrt(v + 1e-8) + 0.1 * w
    return (w - 0.02 * step).astype(BF16), m, v


def clipped(gradients, sum_of_squares, count):
    factor = jnp.minimum(1.0, 0.5 * lax.rsqrt(sum_of_squares / count + 1e-30))
    return [g * factor for g in gradients]


def solution(mesh):
    def step(x, dy, *arrays):
        weights, m, v = (arrays[i : i + 3] for i in (0, 3, 6))
        (g0, g1), (u0, u1), (d0, d1) = ((w[0], w[1]) for w in weights)
        wide, deep = g0.shape, d0.shape
        x, dy = x[0], dy[0]

        a0 = scaled(x)
        wg0, wu0 = alone("gather", carried=Gather([wide, wide], 2), carried_args=(g0, u0), number=1)
        (act0, s0, v0), (wd0,) = up_kernel(a0, wg0, wu0, carried=Gather([deep], 2), carried_args=(d0,), number=2)
        (h1, a1), (wg1, wu1) = down_kernel(act0, wd0, x, carried=Gather([wide, wide], 2), carried_args=(g1, u1), number=3)
        (act1, s1, v1), (wd1,) = up_kernel(a1, wg1, wu1, carried=Gather([deep], 2), carried_args=(d1,), number=4)

        (by_g, by_u, by_d1, by_g1, by_u1), _ = back_kernel(a1.T, dy, wd1, act1, s1, v1, True)
        (dh,), (sd1,) = through_kernel(by_g, by_u, wg1, wu1, h1, dy, carried=Scatter([deep], 2), carried_args=(by_d1,), number=5)
        (by_d0, by_g0, by_u0), (sg1, su1) = back_kernel(
            a0.T, dh, wd0, act0, s0, v0, False, carried=Scatter([wide, wide], 2), carried_args=(by_g1, by_u1), number=6
        )
        sd0, sg0, su0 = alone("scatter", carried=Scatter([deep, wide, wide], 2), carried_args=(by_d0, by_g0, by_u0), number=7)

        mine = ((sg0, sg1), (su0, su1), (sd0, sd1))
        gradients = [jnp.stack(pair).astype(F32) for pair in mine]
        squares = lax.psum(sum(jnp.sum(g * g) for g in gradients), "dp")
        gradients = clipped(gradients, squares, lax.psum(1, "dp") * sum(g.size for g in gradients))
        new = [adamw(w.astype(F32), m, v, g) for w, m, v, g in zip(weights, m, v, gradients, strict=True)]
        return tuple(one[which] for which in range(3) for one in new)

    states, cut = P(("rep", "dp"), None, None), P(None, "dp", None)
    return jax.shard_map(
        step,
        mesh=mesh,
        in_specs=(states, states) + (cut,) * 9,
        out_specs=(P("rep", "dp", None),) * 9,
        check_vma=False,
    )
```

time: 1130 us -> 677 us (0.60)
  waiting for transfers between devices: 646 us -> 0 us
  Pallas kernels: 0 us -> 585 us
  matrix products: 378 us -> 0 us
  between operations: 17.5 us -> 3.93 us
    pallas_call x0 -> x8, Pallas kernels: none -> 585 us  [hosted(): pl.pallas_call(kernel, grid=(steps,), in_specs=[*in_specs, *[ANY] * n_cin...]
    reduce_scatter x6 -> x0, waiting for transfers between devices: 389 us -> none  [step(): lax.psum_scatter(by_w[name], 'dp', scatter_dimension=0, tiled=True)]
    dot_general x15 -> x0, matrix products: 378 us -> none  [the longest x5 137 us: layer(): gate = jnp.dot(a, w['w_gate'], preferred_element_type=jnp.float32)]
    all_gather x6 -> x0, waiting for transfers between devices: 255 us -> none  [fetched(): lax.all_gather(w[number], 'dp', axis=0, tiled=True)]
  transfers between devices with their start and end apart: 12 -> 0, of which waited for: 11 -> 0; matrix products, arithmetic and copies ran while one was open for 27% -> 0% of each run, Pallas kernels for 0% -> 0%
where the time goes in v1:
time: 677 us; the launch traced here: 671 us
  Pallas kernels  585 us (86%)
  blocking collectives  33.1 us (5%)
  other arithmetic  24.9 us (4%)
  local copies, waits for them, and re-layouts  24.1 us (4%)
    pallas_call x8, Pallas kernels, hosted(): pl.pallas_call(kernel, grid=(steps,), in_specs=[*in_specs, *[ANY] * n_cin...  585 us
    psum x1, blocking collectives, step(): squares = lax.psum(sum((jnp.sum(g * g) for g in gradients)), 'dp')  33.1 us

profile of v1, /device:TPU:0, one launch (start us, length us, event | category | flops | bytes accessed | tf_op | source)
XLA Modules:
  0.0 671.1 jit_solution(15571690401474464793)
XLA Ops:
  0.7 2.2 slice_bitcast_fusion
  2.9 1.2 slice_bitcast_fusion.1
  4.1 6.5 copy.20
  10.6 3.2 fusion
  13.8 0.2 copy-done
  14.0 3.3 fusion.29.refs_0_
  17.3 3.2 fusion.1
  20.5 6.4 copy.21.refs_0_
  27.0 71.2 %gather.1 = (bf16[1024,3328]{1,0:T(8,128)(2,1)}, bf16[1024,3328]{1,0:T(8,128)(2,1)}) custom-call(bf16[64,3328]{1,0:T(8,128)(2,1)} %get-tuple-element.82.refs_0_, bf16[64,3328]{1,0:T(8,128)(2,1)} %get-tuple-element.79.refs_1_), custom_call_target="tpu_custom_call" | custom-call | tf_op jit(solution)/shard_map/gather/pallas_call | solution.py:269
  98.2 51.2 %up.2 = (bf16[2048,3328]{1,0:T(8,128)(2,1)}, f32[2048,3328]{1,0:T(8,128)}, f32[2048,3328]{1,0:T(8,128)}, bf16[3328,1024]{1,0:T(8,128)(2,1)}) custom-call(bf16[2048,1024]{1,0:T(8,128)(2,1)} %copy.21.refs_0_, bf16[1024,3328]{1,0:T(8,128)(2,1)} %get-tuple-element.38.refs_1_, bf16[1024,3328]{1,0:T(8,128)(2,1)} %get-tuple-element.39.refs_2_, ...), custom_call_target="tpu_custom_call" | custom-call | tf_op jit(solution)/shard_map/up/pallas_call | solution.py:269
  149.4 77.8 %down.1 = (bf16[2048,1024]{1,0:T(8,128)(2,1)}, bf16[2048,1024]{1,0:T(8,128)(2,1)}, bf16[1024,3328]{1,0:T(8,128)(2,1)}, bf16[1024,3328]{1,0:T(8,128)(2,1)}) custom-call(bf16[2048,3328]{1,0:T(8,128)(2,1)} %get-tuple-element.40.refs_0_.refs_3_, bf16[3328,1024]{1,0:T(8,128)(2,1)} %get-tuple-element.41.refs_1_.refs_2_, bf16[2048,1024]{1,0:T(8,128)(2,1)} %bitcast.28, ...), custom_call_target="tpu_custom_call" | custom-call | tf_op jit(solution)/shard_map/down/pallas_call | solution.py:269
  227.2 6.5 copy.23
  233.7 50.2 %up.3 = (bf16[2048,3328]{1,0:T(8,128)(2,1)}, f32[2048,3328]{1,0:T(8,128)}, f32[2048,3328]{1,0:T(8,128)}, bf16[3328,1024]{1,0:T(8,128)(2,1)}) custom-call(bf16[2048,1024]{1,0:T(8,128)(2,1)} %get-tuple-element.42.refs_0_, bf16[1024,3328]{1,0:T(8,128)(2,1)} %get-tuple-element.43.refs_1_.refs_2_, bf16[1024,3328]{1,0:T(8,128)(2,1)} %get-tuple-element.44.refs_2_.refs_3_, ...), custom_call_target="tpu_custom_call" | custom-call | tf_op jit(solution)/shard_map/up/pallas_call | solution.py:269
  283.8 68.3 %back.2 = (bf16[2048,3328]{1,0:T(8,128)(2,1)}, bf16[2048,3328]{1,0:T(8,128)(2,1)}, bf16[3328,1024]{1,0:T(8,128)(2,1)}, bf16[1024,3328]{1,0:T(8,128)(2,1)}, bf16[1024,3328]{1,0:T(8,128)(2,1)}) custom-call(bf16[1024,2048]{1,0:T(8,128)(2,1)} %bitcast.29, bf16[2048,1024]{1,0:T(8,128)(2,1)} %bitcast.30, bf16[3328,1024]{1,0:T(8,128)(2,1)} %get-tuple-element.45.refs_2_, ...), custom_call_target="tpu_custom_call" | custom-call | tf_op jit(solution)/shard_map/back/pallas_call | solution.py:269
  352.2 51.9 %through.1 = (bf16[2048,1024]{1,0:T(8,128)(2,1)}, bf16[208,1024]{1,0:T(8,128)(2,1)}) custom-call(bf16[2048,3328]{1,0:T(8,128)(2,1)} %get-tuple-element.49.refs_0_, bf16[2048,3328]{1,0:T(8,128)(2,1)} %get-tuple-element.50.refs_1_, bf16[1024,3328]{1,0:T(8,128)(2,1)} %get-tuple-element.43.refs_1_.refs_2_, bf16[1024,3328]{1,0:T(8,128)(2,1)} %get-tuple-element.44.refs_2_.refs_3_, ...), custom_call_target="tpu_custom_call" | custom-call | tf_op jit(solution)/shard_map/through/pallas_call | solution.py:269
  404.0 110.7 %back.3 = (bf16[3328,1024]{1,0:T(8,128)(2,1)}, bf16[1024,3328]{1,0:T(8,128)(2,1)}, bf16[1024,3328]{1,0:T(8,128)(2,1)}, bf16[64,3328]{1,0:T(8,128)(2,1)}, bf16[64,3328]{1,0:T(8,128)(2,1)}) custom-call(bf16[1024,2048]{1,0:T(8,128)(2,1)} %fusion.29.refs_0_, bf16[2048,1024]{1,0:T(8,128)(2,1)} %get-tuple-element.53.refs_1_, ...), custom_call_target="tpu_custom_call" | custom-call | tf_op jit(solution)/shard_map/back/pallas_call | solution.py:269
  514.8 103.8 %scatter.1 = (bf16[208,1024]{1,0:T(8,128)(2,1)}, bf16[64,3328]{1,0:T(8,128)(2,1)}, bf16[64,3328]{1,0:T(8,128)(2,1)}) custom-call(bf16[3328,1024]{1,0:T(8,128)(2,1)} %get-tuple-element.58.refs_0_, bf16[1024,3328]{1,0:T(8,128)(2,1)} %get-tuple-element.59.refs_1_, bf16[1024,3328]{1,0:T(8,128)(2,1)} %get-tuple-element.60.refs_2_), custom_call_target="tpu_custom_call" | custom-call | tf_op jit(solution)/shard_map/scatter/pallas_call | solution.py:269
  618.6 0.0 copy-start.8
  618.6 0.0 copy-start.1
  618.6 2.2 fusion.13
  620.8 2.0 fusion.11
  622.9 1.0 fusion.12
  625.8 33.1 %psum.7 = f32[]{:T(128)} all-reduce(f32[]{:T(128)S(6)} %add.64), channel_id=1, replica_groups=mesh['rep'=2,'dp'=16] {'dp'}, use_global_device_ids=true, to_apply=%region_4.0 | all-reduce | flops 1 | bytes 8 | tf_op jit(solution)/shard_map/psum | solution.py:439
  659.7 0.0 copy-start.4
  659.7 0.0 copy-start.5
  659.7 4.9 fusion.19
  664.6 0.0 copy-start.6
  664.7 0.0 copy-start.7
  664.7 2.5 fusion.10
  667.2 0.9 copy-done.7
  668.1 0.1 copy-done.13
  668.2 2.5 fusion.16
  (22 shorter events, 0.1 us)
Async XLA Ops:
  0.6 2.2 copy-start.3
  0.7 2.2 copy-start.2
  10.6 3.4 copy-start
  514.7 103.9 %copy-start.9 = (bf16[208,1024]{1,0:T(8,128)(2,1)S(1)}, bf16[208,1024]{1,0:T(8,128)(2,1)}, u32[]{:S(2)}) copy-start(bf16[208,1024]{1,0:T(8,128)(2,1)} %get-tuple-element.66) | copy-start | bytes 1277956
  514.8 106.1 %copy-start.10 = (bf16[64,3328]{1,0:T(8,128)(2,1)S(1)}, bf16[64,3328]{1,0:T(8,128)(2,1)}, u32[]{:S(2)}) copy-start(bf16[64,3328]{1,0:T(8,128)(2,1)} %get-tuple-element.62) | copy-start | bytes 1277956
  618.6 4.3 copy-start.8
  618.6 4.3 copy-start.12
  618.6 41.1 %copy-start.1 = (bf16[2,208,1024]{2,1,0:T(8,128)(2,1)S(1)}, bf16[2,208,1024]{2,1,0:T(8,128)(2,1)}, u32[]{:S(2)}) copy-start(bf16[2,208,1024]{2,1,0:T(8,128)(2,1)} %param.15) | copy-start | bytes 2555908
  659.7 4.9 copy-start.4
  659.7 4.9 copy-start.5
  659.7 4.9 copy-start.11
  659.7 4.9 copy-start.14
  664.6 2.6 copy-start.6
  664.7 3.5 copy-start.7
  664.7 3.5 copy-start.13

commit v2 on v1

--- a/solution.py
+++ b/solution.py
@@ -24,6 +24,8 @@
         self.p = order(lax.div(me, 2))
         self.sibling = {"dp": 2 * lax.div(me, 2) + 1 - self.c}
         self.hops = (4 - self.c, 3 + self.c)
+        self.rep = lax.axis_index("rep")
+        self.twin = {"rep": 1 - self.rep}
         self.next = tuple({"dp": 2 * self.chip(o) + self.c} for o in (1, CHIPS - 1))
 
     def chip(self, offset):
@@ -34,54 +36,64 @@
     return pltpu.make_async_remote_copy(src, dst, send, recv, device_id=to, device_id_type=pl.DeviceIdType.MESH)
 
 
-def greet(here):
+def greet(*others):
     barrier = pltpu.get_barrier_semaphore()
-    for to in (here.sibling, *here.next):
+    for to in others:
         pl.semaphore_signal(barrier, inc=1, device_id=to, device_id_type=pl.DeviceIdType.MESH)
-    pl.semaphore_wait(barrier, 3)
+    pl.semaphore_wait(barrier, len(others))
 
 
 class Gather:
-    def __init__(self, shapes, cuts):
-        self.shapes, self.cuts = shapes, cuts
-        self.units = [(m, i, shape[0], shape[1] // cuts) for m, shape in enumerate(shapes) for i in range(cuts)]
+    def __init__(self, shapes, units, number):
+        self.shapes, self.number = shapes, number
+        self.units = [(m, at, side, ring) for m, at, side, ring in units]
         n = len(self.units)
-        self.rounds = 5 * n
+        self.rounds = 6 * n
         dma = pltpu.SemaphoreType.DMA
-        self.scratch = [dma((n, 2, 4)), dma((n, 2, 4)), dma((n, CHIPS)), dma((n, CHIPS)), dma((len(shapes),))]
+        self.scratch = [dma((n, 2, 4)), dma((n, 2, 4)), *[dma((n, CHIPS))] * 6, dma((len(shapes),))]
         self.scratch += [pltpu.VMEM(shape, BF16) for shape in shapes]
         self.out_shapes = [jax.ShapeDtypeStruct((2 * CHIPS * r, c), BF16) for r, c in shapes]
 
     def bind(self, ins, outs, scratch):
-        self.ins, self.outs = ins, outs
-        self.send, self.recv, self.dsend, self.drecv, self.local = scratch[:5]
-        self.held = scratch[5:]
-
-    def block(self, here, u, offset, core):
-        m, i, rows, cols = self.units[u]
-        start = pl.multiple_of((2 * here.chip(offset) + core) * rows, 16)
-        return self.outs[m].at[pl.ds(start, rows), pl.ds(i * cols, cols)]
-
-    def own(self, u):
-        m, i, rows, cols = self.units[u]
-        return self.ins[m].at[:, pl.ds(i * cols, cols)]
+        self.ins, self.outs = [ref.at[self.number] for ref in ins], outs
+        self.send, self.recv, self.dsend, self.drecv, self.xsend, self.xrecv, self.tsend, self.trecv, self.local = scratch[:9]
+        self.held = scratch[9:]
+
+    def columns(self, here, u, kind):
+        m, at, side, ring = self.units[u]
+        if kind == "all":
+            return pl.ds(at, side + ring)
+        if kind == "ring":
+            return pl.ds(pl.multiple_of(at + here.rep * side, 128), ring)
+        rep = here.rep if kind == "gives" else 1 - here.rep
+        return pl.ds(pl.multiple_of(at + rep * ring, 128), side)
+
+    def block(self, here, u, offset, kind):
+        m = self.units[u][0]
+        rows = self.shapes[m][0]
+        start = pl.multiple_of((2 * here.chip(offset) + here.c) * rows, 16)
+        return self.outs[m].at[pl.ds(start, rows), self.columns(here, u, kind)]
+
+    def own(self, here, u, kind):
+        return self.ins[self.units[u][0]].at[:, self.columns(here, u, kind)]
 
     def start(self, here):
-        greet(here)
+        greet(here.sibling, here.twin, *here.next)
         for m in range(len(self.shapes)):
             pltpu.make_async_copy(self.ins[m], self.held[m], self.local.at[m]).start()
 
     def unit(self, here, u, h):
         @pl.when(h == 0)
         def _():
-            mine, dst = self.own(u), self.block(here, u, 0, here.c)
+            mine, dst = self.own(here, u, "ring"), self.block(here, u, 0, "ring")
             for d in range(2):
                 remote(mine, dst, self.send.at[u, d, 0], self.recv.at[u, d, 0], here.next[d]).start()
+            mine, dst = self.own(here, u, "all"), self.block(here, u, 0, "all")
             remote(mine, dst, self.dsend.at[u, 0], self.drecv.at[u, 0], here.sibling).start()
 
         for d in range(2):
-            offset = lax.rem(CHIPS - h, CHIPS) if d == 0 else h
-            blk = self.block(here, u, offset, here.c)
+            offset = lax.rem(CHIPS - h, CHIPS) if d == 0 else lax.rem(h, CHIPS)
+            blk = self.block(here, u, offset, "ring")
 
             @pl.when((h >= 1) & (h <= here.hops[d]))
             def _():
@@ -93,40 +105,59 @@
 
             @pl.when((h >= 1) & (h <= here.hops[d]))
             def _():
+                part = self.block(here, u, offset, "gives")
+                remote(part, part, self.xsend.at[u, offset], self.xrecv.at[u, offset], here.twin).start()
                 remote(blk, blk, self.dsend.at[u, offset], self.drecv.at[u, offset], here.sibling).start()
+
+        for d in range(2):
+            before = lax.rem(CHIPS + 1 - h, CHIPS) if d == 0 else lax.rem(CHIPS + h - 1, CHIPS)
+
+            @pl.when((h >= 2) & (h - 1 <= here.hops[d]))
+            def _():
+                part = self.block(here, u, before, "gets")
+                remote(part, part, self.xsend.at[u, before], self.xrecv.at[u, before], here.twin).wait_recv()
+                remote(part, part, self.tsend.at[u, before], self.trecv.at[u, before], here.sibling).start()
 
     def round(self, here, r):
         n = len(self.units)
         for u in range(n):
             pl.when(lax.rem(r, n) == u)(functools.partial(self.unit, here, u, lax.div(r, n)))
 
+    def rows(self, here, m):
+        rows = self.shapes[m][0]
+        return self.outs[m].at[pl.ds(pl.multiple_of(here.me * rows, 16), rows), :]
+
     def finish(self, here):
-        for m, (rows, cols) in enumerate(self.shapes):
-            mine = self.outs[m].at[pl.ds(pl.multiple_of(here.me * rows, 16), rows), :]
+        for m in range(len(self.shapes)):
             pltpu.make_async_copy(self.ins[m], self.held[m], self.local.at[m]).wait()
-            pltpu.make_async_copy(self.held[m], mine, self.local.at[m]).start()
+            pltpu.make_async_copy(self.held[m], self.rows(here, m), self.local.at[m]).start()
         for u in range(len(self.units)):
-
-            @pl.loop(0, CHIPS)
+            blk = self.block(here, u, 0, "all")
+            remote(blk, blk, self.dsend.at[u, 0], self.drecv.at[u, 0], here.sibling).wait()
+
+            @pl.loop(1, CHIPS)
             def _(o):
-                blk = self.block(here, u, o, here.c)
+                blk = self.block(here, u, o, "ring")
                 remote(blk, blk, self.dsend.at[u, o], self.drecv.at[u, o], here.sibling).wait()
+                blk = self.block(here, u, o, "gives")
+                remote(blk, blk, self.xsend.at[u, o], self.xrecv.at[u, o], here.twin).wait_send()
+                blk = self.block(here, u, o, "gets")
+                remote(blk, blk, self.tsend.at[u, o], self.trecv.at[u, o], here.sibling).wait()
 
             for d in range(2):
 
                 @pl.loop(0, here.hops[d])
                 def _(h):
-                    blk = self.block(here, u, 0, here.c)
+                    blk = self.block(here, u, 0, "ring")
                     remote(blk, blk, self.send.at[u, d, h], self.recv.at[u, d, h], here.next[d]).wait_send()
 
-        for m, (rows, cols) in enumerate(self.shapes):
-            mine = self.outs[m].at[pl.ds(pl.multiple_of(here.me * rows, 16), rows), :]
-            pltpu.make_async_copy(self.held[m], mine, self.local.at[m]).wait()
+        for m in range(len(self.shapes)):
+            pltpu.make_async_copy(self.held[m], self.rows(here, m), self.local.at[m]).wait()
 
 
 class Scatter:
-    def __init__(self, shapes, cuts):
-        self.shapes, self.cuts = shapes, cuts
+    def __init__(self, shapes, cuts, everyone=False):
+        self.shapes, self.cuts, self.everyone = shapes, cuts, everyone
         self.units = [(m, i, shape[0], shape[1] // cuts) for m, shape in enumerate(shapes) for i in range(cuts)]
         n = len(self.units)
         self.rounds = 5 * n
@@ -134,16 +165,17 @@
         self.scratch = [dma((n, 2, 4)), dma((n, 2, 4)), dma((n, CHIPS)), dma((n, CHIPS)), dma((n, CHIPS))]
         for _, _, rows, cols in self.units:
             self.scratch += [pltpu.VMEM((CHIPS, rows, cols), BF16)] * 2 + [pltpu.VMEM((2, 4, rows, cols), BF16)]
-        self.scratch += [pltpu.VMEM(shape, BF16) for shape in shapes] + [dma((len(shapes),))]
-        self.out_shapes = [jax.ShapeDtypeStruct(shape, BF16) for shape in shapes]
+        self.scratch += [pltpu.VMEM(shape, BF16) for shape in shapes] + [dma((len(shapes) + 1,))]
+        self.scratch += [pltpu.VMEM((8, 128), F32), pltpu.VMEM((2 * CHIPS, 8, 128), F32), dma((2 * CHIPS,)), dma((2 * CHIPS,))]
+        self.out_shapes = [*(jax.ShapeDtypeStruct(shape, BF16) for shape in shapes), jax.ShapeDtypeStruct((8, 128), F32)]
 
     def bind(self, ins, outs, scratch):
         self.ins, self.outs = ins, outs
         self.send, self.recv, self.dsend, self.drecv, self.local = scratch[:5]
         n = len(self.units)
         self.mine, self.theirs, self.came = (scratch[5 + j : 5 + 3 * n : 3] for j in range(3))
-        self.total = scratch[5 + 3 * n : -1]
-        self.put = scratch[-1]
+        self.total = scratch[5 + 3 * n : -5]
+        self.put, self.squares, self.slots, self.psend, self.precv = scratch[-5:]
 
     def term(self, here, u, offset, core):
         m, i, rows, cols = self.units[u]
@@ -157,23 +189,42 @@
         term = self.term(here, u, o, 1 - here.c)
         return remote(term, self.theirs[u].at[o], self.dsend.at[u, o], self.drecv.at[u, o], here.sibling)
 
+    def peer(self, here, j):
+        return {"dp": lax.rem(here.me + j, 2 * CHIPS)}
+
     def start(self, here):
-        greet(here)
-
-        @pl.loop(0, CHIPS)
-        def _(j):
-            odd, half = lax.rem(j, 2), lax.div(j, 2)
-            o = lax.rem((1 - odd) * (4 - half) + odd * (5 + half), CHIPS)
+        if self.everyone:
+            greet(*(self.peer(here, j) for j in range(1, 2 * CHIPS)))
+            pltpu.make_async_copy(self.ins[-1], self.squares, self.put.at[len(self.shapes)]).start()
+        else:
+            greet(here.sibling, *here.next)
+        for k in range(2):
             for u in range(len(self.units)):
+                self.ahead(here, u, k)
+
+    def ahead(self, here, u, k):
+        for d in range(2):
+            far = here.hops[d] - k
+            o = lax.rem(far + CHIPS if d == 0 else CHIPS - far, CHIPS)
+
+            @pl.when(k < here.hops[d])
+            def _():
                 self.give(here, u, o).start()
                 self.fetch(here, u, o).start()
 
     def unit(self, here, u, k):
         m, i, rows, cols = self.units[u]
         mine, theirs, came = self.mine[u], self.theirs[u], self.came[u]
+        self.ahead(here, u, k + 2)
+
+        @pl.when(k == 1)
+        def _():
+            self.give(here, u, 0).start()
+            self.fetch(here, u, 0).start()
+
         for d in range(2):
             far = here.hops[d] - k
-            o = far if d == 0 else CHIPS - far
+            o = lax.rem(far + CHIPS if d == 0 else CHIPS - far, CHIPS)
 
             @pl.when(k < here.hops[d])
             def _():
@@ -210,8 +261,32 @@
             pl.when(lax.rem(r, n) == u)(functools.partial(self.unit, here, u, lax.div(r, n)))
 
     def finish(self, here):
-        for m in range(len(self.shapes)):
+        n = len(self.shapes)
+        for m in range(n):
             pltpu.make_async_copy(self.total[m], self.outs[m], self.put.at[m]).start()
+        squares = 0.0
+        for m in range(n):
+            wide = self.total[m][...].astype(F32)
+            squares += jnp.sum(wide * wide)
+        squares = jnp.full((8, 128), squares, F32)
+        if self.everyone:
+            pltpu.make_async_copy(self.ins[-1], self.squares, self.put.at[n]).wait()
+            self.slots[here.me] = self.squares[...] + squares
+
+            @pl.loop(1, 2 * CHIPS)
+            def _(j):
+                slot = self.slots.at[here.me]
+                remote(slot, slot, self.psend.at[j], self.precv.at[here.me], self.peer(here, j)).start()
+
+            @pl.loop(1, 2 * CHIPS)
+            def _(j):
+                other = lax.rem(here.me + j, 2 * CHIPS)
+                slot = self.slots.at[other]
+                remote(slot, slot, self.psend.at[j], self.precv.at[other], self.peer(here, j)).wait()
+
+            squares = jnp.sum(self.slots[...], axis=0)
+        self.squares[...] = squares
+        pltpu.make_async_copy(self.squares, self.outs[n], self.put.at[n]).start()
         for u in range(len(self.units)):
 
             @pl.loop(0, CHIPS)
@@ -226,8 +301,9 @@
                         self.mine[u].at[0], self.came[u].at[d, k], self.send.at[u, d, k], self.recv.at[u, d, k], here.next[d]
                     ).wait_send()
 
-        for m in range(len(self.shapes)):
+        for m in range(n):
             pltpu.make_async_copy(self.total[m], self.outs[m], self.put.at[m]).wait()
+        pltpu.make_async_copy(self.squares, self.outs[n], self.put.at[n]).wait()
 
 
 def hosted(name, body, steps, marks, in_specs, out_specs, out_shape, args, carried=None, carried_args=(), number=None, scratch=(), limit=60):
@@ -292,14 +368,32 @@
     return (wide * lax.rsqrt(jnp.mean(wide * wide, -1, keepdims=True) + 1e-6)).astype(BF16)
 
 
-def up_kernel(a, wg, wu, **carry):
+def norm_kernel(x, **carry):
+    t, d = x.shape
+    m = 512
+
+    def body(ins, outs, own, mark):
+        a = scaled(ins[0][...])
+        outs[0][...] = a
+        outs[1][...] = a.T
+        mark(0)
+
+    row = pl.BlockSpec((m, d), lambda i: (i, 0))
+    return hosted(
+        "norm", body, t // m, 1, [row], [row, pl.BlockSpec((d, m), lambda i: (0, i))],
+        [jax.ShapeDtypeStruct((t, d), BF16), jax.ShapeDtypeStruct((d, t), BF16)], (x,), **carry,
+    )
+
+
+def up_kernel(a, wg, wu, dy=None, **carry):
     t, d = a.shape
     ff = wg.shape[1]
     n, part = 256, 512
+    last = dy is not None
 
     def body(ins, outs, own, mark):
-        a, wg, wu = ins
-        act, s, v = outs
+        a, wg, wu = ins[:3]
+        act, s, v = (*own, *outs[:2]) if last else outs
         for j in range(t // part):
             rows = pl.ds(j * part, part)
             g = dot(a[rows, :], wg[...], (1, 0))
@@ -309,12 +403,18 @@
             act[rows, :] = (sl * u).astype(BF16)
             s[rows, :] = sl
             v[rows, :] = u * (sig * (1.0 + g * (1.0 - sig)))
-            mark(j)
+        if last:
+            outs[2][...] = dot(act[...], ins[3][...], (0, 0)).astype(BF16)
+        mark(0)
 
     col = lambda rows: pl.BlockSpec((rows, n), lambda i: (0, i))
+    row = pl.BlockSpec((n, d), lambda i: (i, 0))
     return hosted(
-        "up", body, ff // n, t // part, [whole((t, d)), col(d), col(d)], [col(t)] * 3,
-        [jax.ShapeDtypeStruct((t, ff), x) for x in (BF16, F32, F32)], (a, wg, wu), **carry,
+        "up", body, ff // n, 1, [whole((t, d)), col(d), col(d)] + [whole((t, d))] * last,
+        [col(t)] * 2 + [row] if last else [col(t)] * 3,
+        [jax.ShapeDtypeStruct((t, ff), F32)] * 2 + [jax.ShapeDtypeStruct((ff, d), BF16)]
+        if last else [jax.ShapeDtypeStruct((t, ff), x) for x in (BF16, F32, F32)],
+        (a, wg, wu) + (dy,) * last, scratch=[pltpu.VMEM((t, n), BF16)] * last, **carry,
     )
 
 
@@ -325,49 +425,69 @@
 
     def body(ins, outs, own, mark):
         act, wd, h = ins
-        new, a = outs
+        new, a, at = outs
         for j in range(d // n):
             cols = pl.ds(j * n, n)
             new[:, cols] = h[:, cols] + dot(act[...], wd[:, cols], (1, 0)).astype(BF16)
             mark(j)
         a[...] = scaled(new[...])
+        at[...] = a[...].T
 
     row = lambda cols: pl.BlockSpec((m, cols), lambda i: (i, 0))
     return hosted(
-        "down", body, t // m, d // n, [row(ff), whole((ff, d)), row(d)], [row(d)] * 2,
-        [jax.ShapeDtypeStruct((t, d), BF16)] * 2, (act, wd, h), **carry,
-    )
-
-
-def back_kernel(at, dh, wd, act, s, v, keep, **carry):
-    d, t = at.shape
-    ff = act.shape[1]
+        "down", body, t // m, d // n, [row(ff), whole((ff, d)), row(d)], [row(d)] * 2 + [pl.BlockSpec((d, m), lambda i: (0, i))],
+        [jax.ShapeDtypeStruct((t, d), BF16)] * 2 + [jax.ShapeDtypeStruct((d, t), BF16)], (act, wd, h), **carry,
+    )
+
+
+def back_kernel(dh, wd, s, v, act=None, at=None, **carry):
+    t, d = dh.shape
+    ff = s.shape[1]
     n, part = 256, 512
+    down = act is not None
 
     def body(ins, outs, own, mark):
-        at, dh, wd, act, s, v = ins
-        by_g, by_u, by_wd, by_wg, by_wu = outs if keep else (*own, *outs)
+        dh, wd, s, v, other = ins
+        by_g, by_u = outs[:2]
         for j in range(t // part):
             rows = pl.ds(j * part, part)
             by_act = dot(dh[rows, :], wd[...], (1, 1)).astype(BF16).astype(F32)
             by_g[rows, :] = (by_act * v[rows, :]).astype(BF16)
             by_u[rows, :] = (by_act * s[rows, :]).astype(BF16)
         mark(0)
-        by_wd[...] = dot(act[...], dh[...], (0, 0)).astype(BF16)
+        if down:
+            outs[2][...] = dot(other[...], dh[...], (0, 0)).astype(BF16)
+        else:
+            outs[2][...] = dot(other[...], by_g[...], (1, 0)).astype(BF16)
+            outs[3][...] = dot(other[...], by_u[...], (1, 0)).astype(BF16)
         mark(1)
-        by_wg[...] = dot(at[...], by_g[...], (1, 0)).astype(BF16)
-        mark(2)
-        by_wu[...] = dot(at[...], by_u[...], (1, 0)).astype(BF16)
-        mark(3)
 
     col = lambda rows: pl.BlockSpec((rows, n), lambda i: (0, i))
     row = pl.BlockSpec((n, d), lambda i: (i, 0))
     shape = lambda *s: jax.ShapeDtypeStruct(s, BF16)
     return hosted(
-        "back", body, ff // n, 4, [whole((d, t)), whole((t, d)), row, col(t), col(t), col(t)],
-        [col(t)] * (2 * keep) + [row, col(d), col(d)],
-        [shape(t, ff)] * (2 * keep) + [shape(ff, d), shape(d, ff), shape(d, ff)],
-        (at, dh, wd, act, s, v), scratch=() if keep else [pltpu.VMEM((t, n), BF16)] * 2, **carry,
+        "back", body, ff // n, 2, [whole((t, d)), row, col(t), col(t), col(t) if down else whole((d, t))],
+        [col(t)] * 2 + ([row] if down else [col(d)] * 2),
+        [shape(t, ff)] * 2 + ([shape(ff, d)] if down else [shape(d, ff)] * 2),
+        (dh, wd, s, v, act if down else at), **carry,
+    )
+
+
+def outer_kernel(at, by_g, by_u, **carry):
+    d, t = at.shape
+    ff = by_g.shape[1]
+    n = 256
+
+    def body(ins, outs, own, mark):
+        at, by_g, by_u = ins
+        for by, out in ((by_g, outs[0]), (by_u, outs[1])):
+            out[...] = dot(at[...], by[...], (1, 0)).astype(BF16)
+        mark(0)
+
+    col = lambda rows: pl.BlockSpec((rows, n), lambda i: (0, i))
+    return hosted(
+        "outer", body, ff // n, 1, [whole((d, t)), col(t), col(t)], [col(d)] * 2, [jax.ShapeDtypeStruct((d, ff), BF16)] * 2,
+        (at, by_g, by_u), **carry,
     )
 
 
@@ -417,27 +537,32 @@
 def solution(mesh):
     def step(x, dy, *arrays):
         weights, m, v = (arrays[i : i + 3] for i in (0, 3, 6))
-        (g0, g1), (u0, u1), (d0, d1) = ((w[0], w[1]) for w in weights)
-        wide, deep = g0.shape, d0.shape
+        w_gate, w_up, w_down = weights
+        wide, deep = w_gate.shape[1:], w_down.shape[1:]
         x, dy = x[0], dy[0]
 
-        a0 = scaled(x)
-        wg0, wu0 = alone("gather", carried=Gather([wide, wide], 2), carried_args=(g0, u0), number=1)
-        (act0, s0, v0), (wd0,) = up_kernel(a0, wg0, wu0, carried=Gather([deep], 2), carried_args=(d0,), number=2)
-        (h1, a1), (wg1, wu1) = down_kernel(act0, wd0, x, carried=Gather([wide, wide], 2), carried_args=(g1, u1), number=3)
-        (act1, s1, v1), (wd1,) = up_kernel(a1, wg1, wu1, carried=Gather([deep], 2), carried_args=(d1,), number=4)
-
-        (by_g, by_u, by_d1, by_g1, by_u1), _ = back_kernel(a1.T, dy, wd1, act1, s1, v1, True)
-        (dh,), (sd1,) = through_kernel(by_g, by_u, wg1, wu1, h1, dy, carried=Scatter([deep], 2), carried_args=(by_d1,), number=5)
-        (by_d0, by_g0, by_u0), (sg1, su1) = back_kernel(
-            a0.T, dh, wd0, act0, s0, v0, False, carried=Scatter([wide, wide], 2), carried_args=(by_g1, by_u1), number=6
-        )
-        sd0, sg0, su0 = alone("scatter", carried=Scatter([deep, wide, wide], 2), carried_args=(by_d0, by_g0, by_u0), number=7)
+        tile = 128
+        pair = [(m, at * tile, side * tile, (13 - side) * tile) for m in range(2) for at, side in ((0, 4), (13, 5))]
+        single = [(0, at * tile, side * tile, (4 - side) * tile) for at, side in ((0, 1), (4, 2))]
+        two = lambda layer, number: dict(carried=Gather([wide, wide], pair, layer), carried_args=(w_gate, w_up), number=number)
+        one = lambda layer, number: dict(carried=Gather([deep], single, layer), carried_args=(w_down,), number=number)
+        total = lambda shape, by, number: dict(carried=Scatter([shape], 2), carried_args=(by,), number=number)
+
+        (a0, at0), (wg0, wu0) = norm_kernel(x, **two(0, 1))
+        (act0, s0, v0), (wd0,) = up_kernel(a0, wg0, wu0, **one(0, 2))
+        (h1, a1, at1), (wg1, wu1) = down_kernel(act0, wd0, x, **two(1, 3))
+        (s1, v1, by_d1), (wd1,) = up_kernel(a1, wg1, wu1, dy, **one(1, 4))
+
+        (by_g, by_u, by_g1, by_u1), (sd1, q1) = back_kernel(dy, wd1, s1, v1, at=at1, **total(deep, by_d1, 5))
+        (dh,), (sg1, q2) = through_kernel(by_g, by_u, wg1, wu1, h1, dy, **total(wide, by_g1, 6))
+        (by_g, by_u, by_d0), (su1, q3) = back_kernel(dh, wd0, s0, v0, act=act0, **total(wide, by_u1, 7))
+        (by_g0, by_u0), (sd0, q4) = outer_kernel(at0, by_g, by_u, **total(deep, by_d0, 8))
+        last = Scatter([wide, wide], 2, everyone=True)
+        sg0, su0, squares = alone("scatter", carried=last, carried_args=(by_g0, by_u0, q1 + q2 + q3 + q4), number=9)
 
         mine = ((sg0, sg1), (su0, su1), (sd0, sd1))
         gradients = [jnp.stack(pair).astype(F32) for pair in mine]
-        squares = lax.psum(sum(jnp.sum(g * g) for g in gradients), "dp")
-        gradients = clipped(gradients, squares, lax.psum(1, "dp") * sum(g.size for g in gradients))
+        gradients = clipped(gradients, squares[0, 0], lax.psum(1, "dp") * sum(g.size for g in gradients))
         new = [adamw(w.astype(F32), m, v, g) for w, m, v, g in zip(weights, m, v, gradients, strict=True)]
         return tuple(one[which] for which in range(3) for one in new)
 

time: 677 us -> 551 us (0.81)
  Pallas kernels: 585 us -> 527 us
  blocking collectives: 33.1 us -> 0 us
  local copies, waits for them, and re-layouts: 24.1 us -> 2.55 us
  other arithmetic: 24.9 us -> 10.9 us
    pallas_call x8 -> x9, Pallas kernels: 585 us -> 527 us  [hosted(): pl.pallas_call(kernel, grid=(steps,), in_specs=[*in_specs, *[ANY] * n_cin...]
    psum x1 -> x0, blocking collectives: 33.1 us -> none  [step(): squares = lax.psum(sum((jnp.sum(g * g) for g in gradients)), 'dp')]
    reduce_sum x4 -> x0, other arithmetic: 8.47 us -> none  [the longest x3 5.26 us: step(): squares = lax.psum(sum((jnp.sum(g * g) for g in gradients)), 'dp')]
where the time goes in v2:
time: 551 us; the launch traced here: 543 us
  Pallas kernels  527 us (96%)
  other arithmetic  10.9 us (2%)
    pallas_call x9, Pallas kernels, hosted(): pl.pallas_call(kernel, grid=(steps,), in_specs=[*in_specs, *[ANY] * n_cin...  527 us

profile of v2, /device:TPU:0, one launch (start us, length us, event | category | flops | bytes accessed | tf_op | source)
XLA Modules:
  0.0 542.9 jit_solution(17170534394091833909)
XLA Ops:
  0.6 61.8 %norm.1 = (bf16[2048,1024]{1,0:T(8,128)(2,1)}, bf16[1024,2048]{1,0:T(8,128)(2,1)}, bf16[1024,3328]{1,0:T(8,128)(2,1)}, bf16[1024,3328]{1,0:T(8,128)(2,1)}) custom-call(bf16[2048,1024]{1,0:T(8,128)(2,1)} %bitcast.12, bf16[2,64,3328]{2,1,0:T(8,128)(2,1)} %refs_3_.3, bf16[2,64,3328]{2,1,0:T(8,128)(2,1)} %refs_4_.2), custom_call_target="tpu_custom_call" | custom-call | tf_op jit(solution)/shard_map/norm/pallas_call | solution.py:345
  62.5 48.6 %up.2 = (bf16[2048,3328]{1,0:T(8,128)(2,1)}, f32[2048,3328]{1,0:T(8,128)}, f32[2048,3328]{1,0:T(8,128)}, bf16[3328,1024]{1,0:T(8,128)(2,1)}) custom-call(bf16[2048,1024]{1,0:T(8,128)(2,1)} %get-tuple-element.48.refs_0_, bf16[1024,3328]{1,0:T(8,128)(2,1)} %get-tuple-element.49.refs_1_, bf16[1024,3328]{1,0:T(8,128)(2,1)} %get-tuple-element.50.refs_2_, ...), custom_call_target="tpu_custom_call" | custom-call | tf_op jit(solution)/shard_map/up/pallas_call | solution.py:345
  111.1 66.2 %down.1 = (bf16[2048,1024]{1,0:T(8,128)(2,1)}, bf16[2048,1024]{1,0:T(8,128)(2,1)}, bf16[1024,2048]{1,0:T(8,128)(2,1)}, bf16[1024,3328]{1,0:T(8,128)(2,1)}, bf16[1024,3328]{1,0:T(8,128)(2,1)}) custom-call(bf16[2048,3328]{1,0:T(8,128)(2,1)} %get-tuple-element.51.refs_0_.refs_4_, bf16[3328,1024]{1,0:T(8,128)(2,1)} %get-tuple-element.52.refs_1_, ...), custom_call_target="tpu_custom_call" | custom-call | tf_op jit(solution)/shard_map/down/pallas_call | solution.py:345
  177.3 58.5 %up.3 = (f32[2048,3328]{1,0:T(8,128)}, f32[2048,3328]{1,0:T(8,128)}, bf16[3328,1024]{1,0:T(8,128)(2,1)}, bf16[3328,1024]{1,0:T(8,128)(2,1)}) custom-call(bf16[2048,1024]{1,0:T(8,128)(2,1)} %get-tuple-element.53.refs_0_, bf16[1024,3328]{1,0:T(8,128)(2,1)} %get-tuple-element.54.refs_1_.refs_2_, bf16[1024,3328]{1,0:T(8,128)(2,1)} %get-tuple-element.55.refs_2_.refs_3_, ...), custom_call_target="tpu_custom_call" | custom-call | tf_op jit(solution)/shard_map/up/pallas_call | solution.py:345
  235.8 62.6 %back.2 = (bf16[2048,3328]{1,0:T(8,128)(2,1)}, bf16[2048,3328]{1,0:T(8,128)(2,1)}, bf16[1024,3328]{1,0:T(8,128)(2,1)}, bf16[1024,3328]{1,0:T(8,128)(2,1)}, bf16[208,1024]{1,0:T(8,128)(2,1)}, /*index=5*/f32[8,128]{1,0:T(8,128)}) custom-call(bf16[2048,1024]{1,0:T(8,128)(2,1)} %bitcast.10, bf16[3328,1024]{1,0:T(8,128)(2,1)} %get-tuple-element.56.refs_1_, ...), custom_call_target="tpu_custom_call" | custom-call | tf_op jit(solution)/shard_map/back/pallas_call | solution.py:345
  298.4 52.9 %through.1 = (bf16[2048,1024]{1,0:T(8,128)(2,1)}, bf16[64,3328]{1,0:T(8,128)(2,1)}, f32[8,128]{1,0:T(8,128)}) custom-call(bf16[2048,3328]{1,0:T(8,128)(2,1)} %get-tuple-element.61.refs_0_, bf16[2048,3328]{1,0:T(8,128)(2,1)} %get-tuple-element.62.refs_1_, bf16[1024,3328]{1,0:T(8,128)(2,1)} %get-tuple-element.54.refs_1_.refs_2_, ...), custom_call_target="tpu_custom_call" | custom-call | tf_op jit(solution)/shard_map/through/pallas_call | solution.py:345
  351.3 52.6 %back.3 = (bf16[2048,3328]{1,0:T(8,128)(2,1)}, bf16[2048,3328]{1,0:T(8,128)(2,1)}, bf16[3328,1024]{1,0:T(8,128)(2,1)}, bf16[64,3328]{1,0:T(8,128)(2,1)}, f32[8,128]{1,0:T(8,128)}) custom-call(bf16[2048,1024]{1,0:T(8,128)(2,1)} %get-tuple-element.65.refs_0_, bf16[3328,1024]{1,0:T(8,128)(2,1)} %get-tuple-element.52.refs_1_, ...), custom_call_target="tpu_custom_call" | custom-call | tf_op jit(solution)/shard_map/back/pallas_call | solution.py:345
  403.9 0.0 copy-start.12
  403.9 0.0 copy-start.13
  403.9 0.0 copy-start.14
  403.9 46.0 %outer.1 = (bf16[1024,3328]{1,0:T(8,128)(2,1)}, bf16[1024,3328]{1,0:T(8,128)(2,1)}, bf16[208,1024]{1,0:T(8,128)(2,1)}, f32[8,128]{1,0:T(8,128)}) custom-call(bf16[1024,2048]{1,0:T(8,128)(2,1)} %get-tuple-element.47.refs_0_, bf16[2048,3328]{1,0:T(8,128)(2,1)} %get-tuple-element.69.refs_1_, bf16[2048,3328]{1,0:T(8,128)(2,1)} %get-tuple-element.70.refs_2_, ...), custom_call_target="tpu_custom_call" | custom-call | tf_op jit(solution)/shard_map/outer/pallas_call | solution.py:345
  449.9 0.0 copy-done.12
  449.9 0.0 copy-done.13
  449.9 0.0 copy-done.14
  449.9 1.3 add_add_fusion.refs_2_
  451.2 78.2 %scatter.1 = (bf16[64,3328]{1,0:T(8,128)(2,1)}, bf16[64,3328]{1,0:T(8,128)(2,1)}, f32[8,128]{1,0:T(8,128)}) custom-call(bf16[1024,3328]{1,0:T(8,128)(2,1)} %get-tuple-element.72.refs_0_, bf16[1024,3328]{1,0:T(8,128)(2,1)} %get-tuple-element.73.refs_1_, f32[8,128]{1,0:T(8,128)} %add_add_fusion.refs_2_), custom_call_target="tpu_custom_call" | custom-call | tf_op jit(solution)/shard_map/scatter/pallas_call | solution.py:345
  529.4 1.2 slice.3
  531.3 0.0 copy-done
  531.3 0.0 copy-done.3
  531.3 0.0 copy-start.1
  531.4 0.0 copy-start.2
  531.4 0.0 copy-start.4
  531.4 0.0 copy-start.5
  531.4 0.0 copy-start.6
  531.4 0.0 copy-start.7
  531.4 4.3 fusion.8
  535.7 0.0 copy-done.1
  535.7 0.0 copy-done.4
  535.7 1.2 copy-done.7
  536.9 0.0 copy-done.9
  536.9 0.1 copy-done.10
  537.0 5.3 fusion.2
  (11 shorter events, 0.0 us)
Async XLA Ops:
  403.9 46.0 %copy-start.12 = (f32[8,128]{1,0:T(8,128)S(1)}, f32[8,128]{1,0:T(8,128)}, u32[]{:S(2)}) copy-start(f32[8,128]{1,0:T(8,128)} %get-tuple-element.74) | copy-start | bytes 12292
  403.9 46.0 %copy-start.13 = (f32[8,128]{1,0:T(8,128)S(1)}, f32[8,128]{1,0:T(8,128)}, u32[]{:S(2)}) copy-start(f32[8,128]{1,0:T(8,128)} %get-tuple-element.75) | copy-start | bytes 12292
  403.9 46.0 %copy-start.14 = (f32[8,128]{1,0:T(8,128)S(1)}, f32[8,128]{1,0:T(8,128)}, u32[]{:S(2)}) copy-start(f32[8,128]{1,0:T(8,128)} %get-tuple-element.76) | copy-start | bytes 12292
  451.2 80.1 %copy-start = (bf16[2,208,1024]{2,1,0:T(8,128)(2,1)S(1)}, bf16[2,208,1024]{2,1,0:T(8,128)(2,1)}, u32[]{:S(2)}) copy-start(bf16[2,208,1024]{2,1,0:T(8,128)(2,1)} %refs_4_.3) | copy-start | bytes 2555908
  451.2 80.1 %copy-start.3 = (f32[2,208,1024]{2,1,0:T(8,128)S(1)}, f32[2,208,1024]{2,1,0:T(8,128)}, u32[]{:S(2)}) copy-start(f32[2,208,1024]{2,1,0:T(8,128)} %param.21) | copy-start | bytes 5111812
  451.2 80.1 %copy-start.8 = (bf16[208,1024]{1,0:T(8,128)(2,1)S(1)}, bf16[208,1024]{1,0:T(8,128)(2,1)}, u32[]{:S(2)}) copy-start(bf16[208,1024]{1,0:T(8,128)(2,1)} %get-tuple-element.84) | copy-start | bytes 1277956
  451.2 80.1 %copy-start.11 = (bf16[208,1024]{1,0:T(8,128)(2,1)S(1)}, bf16[208,1024]{1,0:T(8,128)(2,1)}, u32[]{:S(2)}) copy-start(bf16[208,1024]{1,0:T(8,128)(2,1)} %get-tuple-element.83) | copy-start | bytes 1277956
  531.3 4.4 copy-start.1
  531.4 4.4 copy-start.2
  531.4 4.3 copy-start.4
  531.4 4.3 copy-start.5
  531.4 4.3 copy-start.6
  531.4 5.5 %copy-start.7 = (f32[2,64,3328]{2,1,0:T(8,128)S(1)}, f32[2,64,3328]{2,1,0:T(8,128)}, u32[]{:S(2)}) copy-start(f32[2,64,3328]{2,1,0:T(8,128)} %param.17) | copy-start | bytes 5111812
  531.4 5.5 %copy-start.9 = (bf16[64,3328]{1,0:T(8,128)(2,1)S(1)}, bf16[64,3328]{1,0:T(8,128)(2,1)}, u32[]{:S(2)}) copy-start(bf16[64,3328]{1,0:T(8,128)(2,1)} %get-tuple-element.79) | copy-start | bytes 1277956
  531.4 5.6 %copy-start.10 = (bf16[64,3328]{1,0:T(8,128)(2,1)S(1)}, bf16[64,3328]{1,0:T(8,128)(2,1)}, u32[]{:S(2)}) copy-start(bf16[64,3328]{1,0:T(8,128)(2,1)} %get-tuple-element.82) | copy-start | bytes 1277956

commit v3 on v2

--- a/solution.py
+++ b/solution.py
@@ -421,13 +421,15 @@
 def down_kernel(act, wd, h, **carry):
     t, ff = act.shape
     d = wd.shape[1]
-    m, n = 512, 256
+    m, n = 512, 512
 
     def body(ins, outs, own, mark):
         act, wd, h = ins
         new, a, at = outs
-        for j in range(d // n):
-            cols = pl.ds(j * n, n)
+
+        @pl.loop(0, d // n)
+        def _(j):
+            cols = pl.ds(pl.multiple_of(j * n, n), n)
             new[:, cols] = h[:, cols] + dot(act[...], wd[:, cols], (1, 0)).astype(BF16)
             mark(j)
         a[...] = scaled(new[...])
@@ -494,14 +496,16 @@
 def through_kernel(by_g, by_u, wg, wu, h, dh, **carry):
     t, ff = by_g.shape
     d = wg.shape[0]
-    m, n = 256, 256
+    m, n = 512, 256
 
     def body(ins, outs, own, mark):
         by_g, by_u, wg, wu, h, dh = ins
         (new,) = outs
         (by_a,) = own
-        for j in range(d // n):
-            cols = pl.ds(j * n, n)
+
+        @pl.loop(0, d // n)
+        def _(j):
+            cols = pl.ds(pl.multiple_of(j * n, n), n)
             one = dot(by_g[...], wg[cols, :], (1, 1)).astype(BF16)
             two = dot(by_u[...], wu[cols, :], (1, 1)).astype(BF16)
             by_a[:, cols] = (one + two).astype(F32)
@@ -542,8 +546,8 @@
         x, dy = x[0], dy[0]
 
         tile = 128
-        pair = [(m, at * tile, side * tile, (13 - side) * tile) for m in range(2) for at, side in ((0, 4), (13, 5))]
-        single = [(0, at * tile, side * tile, (4 - side) * tile) for at, side in ((0, 1), (4, 2))]
+        pair = [(m, at * tile, side * tile, (13 - side) * tile) for m in range(2) for at, side in ((0, 4), (13, 4))]
+        single = [(0, at * tile, side * tile, (4 - side) * tile) for at, side in ((0, 1), (4, 1))]
         two = lambda layer, number: dict(carried=Gather([wide, wide], pair, layer), carried_args=(w_gate, w_up), number=number)
         one = lambda layer, number: dict(carried=Gather([deep], single, layer), carried_args=(w_down,), number=number)
         total = lambda shape, by, number: dict(carried=Scatter([shape], 2), carried_args=(by,), number=number)

time: 551 us -> 539 us (0.978); the launches traced: 543 us -> 539 us
  no operation moved by 1% of the time
where the time goes in v3:
time: 539 us
  Pallas kernels  524 us (97%)
  other arithmetic  10.9 us (2%)
    pallas_call x9, Pallas kernels, hosted(): pl.pallas_call(kernel, grid=(steps,), in_specs=[*in_specs, *[ANY] * n_cin...  524 us

profile of v3, /device:TPU:0, one launch (start us, length us, event | category | flops | bytes accessed | tf_op | source)
XLA Modules:
  0.0 538.8 jit_solution(12176464452987854631)
XLA Ops:
  0.6 60.4 %norm.1 = (bf16[2048,1024]{1,0:T(8,128)(2,1)}, bf16[1024,2048]{1,0:T(8,128)(2,1)}, bf16[1024,3328]{1,0:T(8,128)(2,1)}, bf16[1024,3328]{1,0:T(8,128)(2,1)}) custom-call(bf16[2048,1024]{1,0:T(8,128)(2,1)} %bitcast.12, bf16[2,64,3328]{2,1,0:T(8,128)(2,1)} %refs_3_.3, bf16[2,64,3328]{2,1,0:T(8,128)(2,1)} %refs_4_.2), custom_call_target="tpu_custom_call" | custom-call | tf_op jit(solution)/shard_map/norm/pallas_call | solution.py:345
  61.0 47.9 %up.2 = (bf16[2048,3328]{1,0:T(8,128)(2,1)}, f32[2048,3328]{1,0:T(8,128)}, f32[2048,3328]{1,0:T(8,128)}, bf16[3328,1024]{1,0:T(8,128)(2,1)}) custom-call(bf16[2048,1024]{1,0:T(8,128)(2,1)} %get-tuple-element.48.refs_0_, bf16[1024,3328]{1,0:T(8,128)(2,1)} %get-tuple-element.49.refs_1_, bf16[1024,3328]{1,0:T(8,128)(2,1)} %get-tuple-element.50.refs_2_, ...), custom_call_target="tpu_custom_call" | custom-call | tf_op jit(solution)/shard_map/up/pallas_call | solution.py:345
  109.0 63.5 %down.1 = (bf16[2048,1024]{1,0:T(8,128)(2,1)}, bf16[2048,1024]{1,0:T(8,128)(2,1)}, bf16[1024,2048]{1,0:T(8,128)(2,1)}, bf16[1024,3328]{1,0:T(8,128)(2,1)}, bf16[1024,3328]{1,0:T(8,128)(2,1)}) custom-call(bf16[2048,3328]{1,0:T(8,128)(2,1)} %get-tuple-element.51.refs_0_.refs_4_, bf16[3328,1024]{1,0:T(8,128)(2,1)} %get-tuple-element.52.refs_1_, ...), custom_call_target="tpu_custom_call" | custom-call | tf_op jit(solution)/shard_map/down/pallas_call | solution.py:345
  172.4 58.6 %up.3 = (f32[2048,3328]{1,0:T(8,128)}, f32[2048,3328]{1,0:T(8,128)}, bf16[3328,1024]{1,0:T(8,128)(2,1)}, bf16[3328,1024]{1,0:T(8,128)(2,1)}) custom-call(bf16[2048,1024]{1,0:T(8,128)(2,1)} %get-tuple-element.53.refs_0_, bf16[1024,3328]{1,0:T(8,128)(2,1)} %get-tuple-element.54.refs_1_.refs_2_, bf16[1024,3328]{1,0:T(8,128)(2,1)} %get-tuple-element.55.refs_2_.refs_3_, ...), custom_call_target="tpu_custom_call" | custom-call | tf_op jit(solution)/shard_map/up/pallas_call | solution.py:345
  231.1 62.6 %back.2 = (bf16[2048,3328]{1,0:T(8,128)(2,1)}, bf16[2048,3328]{1,0:T(8,128)(2,1)}, bf16[1024,3328]{1,0:T(8,128)(2,1)}, bf16[1024,3328]{1,0:T(8,128)(2,1)}, bf16[208,1024]{1,0:T(8,128)(2,1)}, /*index=5*/f32[8,128]{1,0:T(8,128)}) custom-call(bf16[2048,1024]{1,0:T(8,128)(2,1)} %bitcast.10, bf16[3328,1024]{1,0:T(8,128)(2,1)} %get-tuple-element.56.refs_1_, ...), custom_call_target="tpu_custom_call" | custom-call | tf_op jit(solution)/shard_map/back/pallas_call | solution.py:345
  293.6 54.1 %through.1 = (bf16[2048,1024]{1,0:T(8,128)(2,1)}, bf16[64,3328]{1,0:T(8,128)(2,1)}, f32[8,128]{1,0:T(8,128)}) custom-call(bf16[2048,3328]{1,0:T(8,128)(2,1)} %get-tuple-element.61.refs_0_, bf16[2048,3328]{1,0:T(8,128)(2,1)} %get-tuple-element.62.refs_1_, bf16[1024,3328]{1,0:T(8,128)(2,1)} %get-tuple-element.54.refs_1_.refs_2_, ...), custom_call_target="tpu_custom_call" | custom-call | tf_op jit(solution)/shard_map/through/pallas_call | solution.py:345
  347.7 52.6 %back.3 = (bf16[2048,3328]{1,0:T(8,128)(2,1)}, bf16[2048,3328]{1,0:T(8,128)(2,1)}, bf16[3328,1024]{1,0:T(8,128)(2,1)}, bf16[64,3328]{1,0:T(8,128)(2,1)}, f32[8,128]{1,0:T(8,128)}) custom-call(bf16[2048,1024]{1,0:T(8,128)(2,1)} %get-tuple-element.65.refs_0_, bf16[3328,1024]{1,0:T(8,128)(2,1)} %get-tuple-element.52.refs_1_, ...), custom_call_target="tpu_custom_call" | custom-call | tf_op jit(solution)/shard_map/back/pallas_call | solution.py:345
  400.3 0.0 copy-start.12
  400.3 0.0 copy-start.13
  400.3 0.0 copy-start.14
  400.3 46.0 %outer.1 = (bf16[1024,3328]{1,0:T(8,128)(2,1)}, bf16[1024,3328]{1,0:T(8,128)(2,1)}, bf16[208,1024]{1,0:T(8,128)(2,1)}, f32[8,128]{1,0:T(8,128)}) custom-call(bf16[1024,2048]{1,0:T(8,128)(2,1)} %get-tuple-element.47.refs_0_, bf16[2048,3328]{1,0:T(8,128)(2,1)} %get-tuple-element.69.refs_1_, bf16[2048,3328]{1,0:T(8,128)(2,1)} %get-tuple-element.70.refs_2_, ...), custom_call_target="tpu_custom_call" | custom-call | tf_op jit(solution)/shard_map/outer/pallas_call | solution.py:345
  446.3 0.0 copy-done.12
  446.3 0.0 copy-done.13
  446.4 0.0 copy-done.14
  446.4 1.3 add_add_fusion.refs_2_
  447.7 78.2 %scatter.1 = (bf16[64,3328]{1,0:T(8,128)(2,1)}, bf16[64,3328]{1,0:T(8,128)(2,1)}, f32[8,128]{1,0:T(8,128)}) custom-call(bf16[1024,3328]{1,0:T(8,128)(2,1)} %get-tuple-element.72.refs_0_, bf16[1024,3328]{1,0:T(8,128)(2,1)} %get-tuple-element.73.refs_1_, f32[8,128]{1,0:T(8,128)} %add_add_fusion.refs_2_), custom_call_target="tpu_custom_call" | custom-call | tf_op jit(solution)/shard_map/scatter/pallas_call | solution.py:345
  525.8 1.2 slice.3
  527.7 0.0 copy-done
  527.7 0.0 copy-done.3
  527.7 0.0 copy-done.8
  527.8 0.0 copy-start.1
  527.8 0.0 copy-start.2
  527.8 0.0 copy-start.4
  527.8 0.0 copy-start.5
  527.8 0.0 copy-start.6
  527.8 0.0 copy-start.7
  527.9 4.3 fusion.8
  532.1 0.0 copy-done.1
  532.2 1.2 copy-done.7
  533.3 0.0 copy-done.9
  533.3 0.1 copy-done.10
  533.5 5.3 fusion.2
  (11 shorter events, 0.0 us)
Async XLA Ops:
  400.3 46.0 %copy-start.12 = (f32[8,128]{1,0:T(8,128)S(1)}, f32[8,128]{1,0:T(8,128)}, u32[]{:S(2)}) copy-start(f32[8,128]{1,0:T(8,128)} %get-tuple-element.74) | copy-start | bytes 12292
  400.3 46.0 %copy-start.13 = (f32[8,128]{1,0:T(8,128)S(1)}, f32[8,128]{1,0:T(8,128)}, u32[]{:S(2)}) copy-start(f32[8,128]{1,0:T(8,128)} %get-tuple-element.75) | copy-start | bytes 12292
  400.3 46.0 %copy-start.14 = (f32[8,128]{1,0:T(8,128)S(1)}, f32[8,128]{1,0:T(8,128)}, u32[]{:S(2)}) copy-start(f32[8,128]{1,0:T(8,128)} %get-tuple-element.76) | copy-start | bytes 12292
  447.6 80.1 %copy-start = (bf16[2,208,1024]{2,1,0:T(8,128)(2,1)S(1)}, bf16[2,208,1024]{2,1,0:T(8,128)(2,1)}, u32[]{:S(2)}) copy-start(bf16[2,208,1024]{2,1,0:T(8,128)(2,1)} %refs_4_.3) | copy-start | bytes 2555908
  447.7 80.1 %copy-start.3 = (f32[2,208,1024]{2,1,0:T(8,128)S(1)}, f32[2,208,1024]{2,1,0:T(8,128)}, u32[]{:S(2)}) copy-start(f32[2,208,1024]{2,1,0:T(8,128)} %param.21) | copy-start | bytes 5111812
  447.7 80.1 %copy-start.8 = (bf16[208,1024]{1,0:T(8,128)(2,1)S(1)}, bf16[208,1024]{1,0:T(8,128)(2,1)}, u32[]{:S(2)}) copy-start(bf16[208,1024]{1,0:T(8,128)(2,1)} %get-tuple-element.84) | copy-start | bytes 1277956
  447.7 80.1 %copy-start.11 = (bf16[208,1024]{1,0:T(8,128)(2,1)S(1)}, bf16[208,1024]{1,0:T(8,128)(2,1)}, u32[]{:S(2)}) copy-start(bf16[208,1024]{1,0:T(8,128)(2,1)} %get-tuple-element.83) | copy-start | bytes 1277956
  527.8 4.4 copy-start.1
  527.8 4.4 copy-start.2
  527.8 4.3 copy-start.4
  527.8 4.3 copy-start.5
  527.8 4.3 copy-start.6
  527.8 5.5 %copy-start.7 = (f32[2,64,3328]{2,1,0:T(8,128)S(1)}, f32[2,64,3328]{2,1,0:T(8,128)}, u32[]{:S(2)}) copy-start(f32[2,64,3328]{2,1,0:T(8,128)} %param.17) | copy-start | bytes 5111812
  527.8 5.5 %copy-start.9 = (bf16[64,3328]{1,0:T(8,128)(2,1)S(1)}, bf16[64,3328]{1,0:T(8,128)(2,1)}, u32[]{:S(2)}) copy-start(bf16[64,3328]{1,0:T(8,128)(2,1)} %get-tuple-element.79) | copy-start | bytes 1277956
  527.9 5.6 %copy-start.10 = (bf16[64,3328]{1,0:T(8,128)(2,1)S(1)}, bf16[64,3328]{1,0:T(8,128)(2,1)}, u32[]{:S(2)}) copy-start(bf16[64,3328]{1,0:T(8,128)(2,1)} %get-tuple-element.82) | copy-start | bytes 1277956
